TPU v7x, 32 devices: a whole 2x2x4 slice. The times are simulated.
32 devices in a mesh: dp: 8 (over z, x), tensor: 4 (over y, core).
Axes of the slice: x: 2, y: 2, z: 4, core: 2. Of those that a mesh axis runs over, the one named last changes fastest.
Arguments:
- tokens: bfloat16 [32, 512, 1024], P(('dp', 'tensor')), may hold values from -6 to 6
- segments: int32 [32, 512], P(('dp', 'tensor')), may hold values from 0 to 1, as said below
- separators: int32 [32, 2], P(('dp', 'tensor')), may hold values from 2 to 511, as said below
- lengths: int32 [32], P(('dp', 'tensor')), may hold values from 128 to 512, as said below
- type_table: bfloat16 [2, 1024], replicated, may hold values from -3 to 3
- qkv_weight: bfloat16 [1024, 3072], replicated, may hold values from -0.25 to 0.25
- qv_bias: bfloat16 [2, 1024], replicated, may hold values from -3 to 3
- out_weight: bfloat16 [1024, 1024], replicated, may hold values from -0.75 to 0.75
- out_bias: bfloat16 [1024], replicated, may hold values from -3 to 3
- gain_one: float32 [1024], replicated, may hold values from 0.5 to 1.5
- shift_one: bfloat16 [1024], replicated, may hold values from -3 to 3
- in_weight: bfloat16 [1024, 4096], P(None, 'tensor'), may hold values from -0.1875 to 0.1875
- in_bias: bfloat16 [4096], P('tensor'), may hold values from -3 to 3
- ffn_weight: bfloat16 [4096, 1024], P('tensor'), may hold values from -0.09375 to 0.09375
- ffn_bias: bfloat16 [1024], replicated, may hold values from -3 to 3
- gain_two: float32 [1024], replicated, may hold values from 0.5 to 1.5
- shift_two: bfloat16 [1024], replicated, may hold values from -3 to 3
- cotangent: bfloat16 [32, 512, 1024], P(('dp', 'tensor')), may hold values from -6 to 6
Outputs:
- activations: bfloat16 [32, 512, 1024], P(('dp', 'tensor'))
- tokens_grad: float32 [32, 512, 1024], P(('dp', 'tensor'))
- qv_bias_grad: float32 [2, 1024], replicated
- out_bias_grad: float32 [1024], replicated
- shift_one_grad: float32 [1024], replicated
- in_bias_grad: float32 [4096], P('tensor')
- ffn_bias_grad: float32 [1024], replicated
- shift_two_grad: float32 [1024], replicated
Inputs may be any that keep to these rules, and one draw needn't show every extreme that they name: `lengths`: some pair has exactly 512 real tokens. `separators`: column 0 is the first separator, from 2 to the pair's length minus 3; column 1 is the pair's length minus 1. `segments`: 0 up to and including the first separator and at padded positions, 1 after it up to the pair's length minus 1.
All inputs are finite; a program needn't handle non-finite values.
Results may differ from a plain program's by a relative error of at most 0.014.
The roundings to bfloat16 on the way count: a program that leaves them out, or rounds other values in their place, can miss the bound.
Values may be sent and summed in bfloat16 or wider, within the bound.
A program may use at most 128 MiB of HBM per device.

v0:
```python
import jax
import jax.numpy as jnp
from jax import lax
from jax.sharding import PartitionSpec as P

HEADS = 16


root_half = 0.7071067811865476
inv_root_tau = 0.3989422804014327
eps_norm = 1e-06


def gelu_erf(value):
    return 0.5 * value * (1.0 + jax.scipy.special.erf(value * root_half))


def gelu_slope(value):
    return 0.5 * (1.0 + jax.scipy.special.erf(value * root_half)) + value * inv_root_tau * jnp.exp(
        -0.5 * value * value
    )


def norm_forward(rows, gain, shift):
    centered = rows - jnp.mean(rows, axis=-1, keepdims=True)
    scale = lax.rsqrt(jnp.mean(centered * centered, axis=-1, keepdims=True) + eps_norm)
    normed = centered * scale
    return (normed * gain + shift, normed, scale)


def norm_backward(grad, normed, scale, gain):
    scaled = grad * gain
    centered = scaled - jnp.mean(scaled, axis=-1, keepdims=True)
    return scale * (centered - normed * jnp.mean(scaled * normed, axis=-1, keepdims=True))


def masked_scores(query, key_rows, valid):
    scale = query.shape[-1] ** (-0.5)
    scores = scale * jnp.einsum("qhd,khd->hqk", query, key_rows, preferred_element_type=jnp.float32)
    return jnp.where(valid[None, None, :], scores, -1e30)


def attend_forward(items):
    query, key_rows, value, valid = items
    scores = masked_scores(query, key_rows, valid)
    top = jnp.max(scores, axis=-1, keepdims=True)
    total_log = top + jnp.log(jnp.sum(jnp.exp(scores - top), axis=-1, keepdims=True))
    probs = jnp.exp(scores - total_log).astype(jnp.bfloat16)
    mixed = jnp.einsum("hqk,khd->qhd", probs, value, preferred_element_type=jnp.float32)
    return (mixed.astype(jnp.bfloat16), total_log)


def attend_backward(items):
    query, key_rows, value, valid, total_log, grad_mixed = items
    scale = query.shape[-1] ** (-0.5)
    probs = jnp.exp(masked_scores(query, key_rows, valid) - total_log)
    grad_probs = jnp.einsum("qhd,khd->hqk", grad_mixed, value, preferred_element_type=jnp.float32)
    inner_sum = jnp.sum(probs * grad_probs, axis=-1, keepdims=True)
    grad_scores = (probs * (grad_probs - inner_sum)).astype(jnp.bfloat16)
    grad_query = scale * jnp.einsum(
        "hqk,khd->qhd", grad_scores, key_rows, preferred_element_type=jnp.float32
    )
    grad_keys = scale * jnp.einsum(
        "hqk,qhd->khd", grad_scores, query, preferred_element_type=jnp.float32
    )
    grad_values = jnp.einsum(
        "hqk,qhd->khd", probs.astype(jnp.bfloat16), grad_mixed, preferred_element_type=jnp.float32
    )
    return (
        grad_query.astype(jnp.bfloat16),
        grad_keys.astype(jnp.bfloat16),
        grad_values.astype(jnp.bfloat16),
    )


def local(
    tokens,
    segments,
    separators,
    lengths,
    type_table,
    qkv_weight,
    qv_bias,
    out_weight,
    out_bias,
    gain_one,
    shift_one,
    in_weight,
    in_bias,
    ffn_weight,
    ffn_bias,
    gain_two,
    shift_two,
    cotangent,
):
    pairs, seq, width = tokens.shape
    flat = pairs * seq
    second = segments.astype(jnp.float32)[..., None]
    table = type_table.astype(jnp.float32)
    embedded = (tokens.astype(jnp.float32) + (1.0 - second) * table[0] + second * table[1]).reshape(
        flat, width
    )
    packed = jnp.dot(embedded.astype(jnp.bfloat16), qkv_weight, preferred_element_type=jnp.float32)
    attn_bias = qv_bias.astype(jnp.float32)
    query = (packed[:, :width] + attn_bias[0]).astype(jnp.bfloat16)
    key_rows = packed[:, width : 2 * width].astype(jnp.bfloat16)
    value = (packed[:, 2 * width :] + attn_bias[1]).astype(jnp.bfloat16)
    shaped = (pairs, seq, HEADS, width // HEADS)
    query = query.reshape(shaped)
    key_rows = key_rows.reshape(shaped)
    value = value.reshape(shaped)
    positions = jnp.arange(seq, dtype=jnp.int32)
    valid = positions[None, :] < lengths[:, None]
    mixed, total_log = lax.map(attend_forward, (query, key_rows, value, valid))
    mixed = mixed.reshape(flat, width)
    branch = jnp.dot(mixed, out_weight, preferred_element_type=jnp.float32) + out_bias.astype(
        jnp.float32
    )
    first, normed_one, scale_one = norm_forward(
        embedded + branch, gain_one, shift_one.astype(jnp.float32)
    )
    first_low = first.astype(jnp.bfloat16)
    in_shift = in_bias.astype(jnp.float32)
    inner = (
        jnp.einsum(
            "psd,df->psf",
            lax.all_gather(first_low.reshape(pairs, seq, width), "tensor", axis=0, tiled=True),
            in_weight,
            preferred_element_type=jnp.float32,
        )
        + in_shift
    )
    hidden = gelu_erf(inner).astype(jnp.bfloat16)
    rows = hidden
    outer = lax.psum_scatter(
        jnp.einsum("psf,fd->psd", rows, ffn_weight, preferred_element_type=jnp.float32),
        "tensor",
        scatter_dimension=0,
        tiled=True,
    ).reshape(flat, width)
    final, normed_two, scale_two = norm_forward(
        first + outer + ffn_bias.astype(jnp.float32), gain_two, shift_two.astype(jnp.float32)
    )
    activations = final.astype(jnp.bfloat16).reshape(pairs, seq, width)
    keep = valid & (positions[None, :] > 0)
    keep = (
        keep
        & (positions[None, :] != separators[:, 0:1])
        & (positions[None, :] != separators[:, 1:2])
    )
    grad_final = (cotangent.astype(jnp.float32) * keep.astype(jnp.float32)[..., None]).reshape(
        flat, width
    )
    grad_shift_two = jnp.sum(grad_final, axis=0)
    grad_second = norm_backward(grad_final, normed_two, scale_two, gain_two)
    grad_ffn = grad_second.astype(jnp.bfloat16)
    grad_ffn_bias = jnp.sum(grad_ffn.astype(jnp.float32), axis=0)
    back = jnp.einsum(
        "psd,fd->psf",
        lax.all_gather(grad_ffn.reshape(pairs, seq, width), "tensor", axis=0, tiled=True),
        ffn_weight,
        preferred_element_type=jnp.float32,
    )
    grad_inner = (back * gelu_slope(inner)).astype(jnp.bfloat16)
    grad_in_part = jnp.sum(grad_inner.astype(jnp.float32), axis=(0, 1))
    grad_in_bias = lax.psum(grad_in_part, "dp")
    rows = grad_inner
    grad_first = lax.psum_scatter(
        jnp.einsum("psf,df->psd", rows, in_weight, preferred_element_type=jnp.float32),
        "tensor",
        scatter_dimension=0,
        tiled=True,
    ).reshape(flat, width)
    grad_first = grad_first + grad_second
    grad_shift_one = jnp.sum(grad_first, axis=0)
    grad_sum_one = norm_backward(grad_first, normed_one, scale_one, gain_one)
    grad_branch = grad_sum_one.astype(jnp.bfloat16)
    grad_out_bias = jnp.sum(grad_branch.astype(jnp.float32), axis=0)
    grad_mixed = jnp.einsum(
        "ne,de->nd", grad_branch, out_weight, preferred_element_type=jnp.float32
    ).astype(jnp.bfloat16)
    grad_query, grad_keys, grad_values = lax.map(
        attend_backward, (query, key_rows, value, valid, total_log, grad_mixed.reshape(shaped))
    )
    grad_query = grad_query.reshape(flat, width)
    grad_keys = grad_keys.reshape(flat, width)
    grad_values = grad_values.reshape(flat, width)
    grad_packed = jnp.concatenate([grad_query, grad_keys, grad_values], axis=1)
    tokens_grad = (
        jnp.einsum("nc,dc->nd", grad_packed, qkv_weight, preferred_element_type=jnp.float32)
        + grad_sum_one
    )
    grad_qv = jnp.stack(
        [
            jnp.sum(grad_query.astype(jnp.float32), axis=0),
            jnp.sum(grad_values.astype(jnp.float32), axis=0),
        ]
    )
    totals = lax.psum(
        (grad_qv, grad_out_bias, grad_shift_one, grad_ffn_bias, grad_shift_two), ("dp", "tensor")
    )
    return (
        activations,
        tokens_grad.reshape(pairs, seq, width),
        totals[0],
        totals[1],
        totals[2],
        grad_in_bias,
        totals[3],
        totals[4],
    )


def solution(mesh):
    return jax.shard_map(
        local,
        mesh=mesh,
        in_specs=(
            P(("dp", "tensor"), None, None),
            P(("dp", "tensor"), None),
            P(("dp", "tensor"), None),
            P(("dp", "tensor")),
            P(),
            P(),
            P(),
            P(),
            P(),
            P(),
            P(),
            P(None, "tensor"),
            P("tensor"),
            P("tensor", None),
            P(),
            P(),
            P(),
            P(("dp", "tensor"), None, None),
        ),
        out_specs=(
            P(("dp", "tensor"), None, None),
            P(("dp", "tensor"), None, None),
            P(),
            P(),
            P(),
            P("tensor"),
            P(),
            P(),
        ),
        check_vma=False,
    )
```

profile of v0, /device:TPU:0, one launch (start us, length us, event | category | flops | bytes accessed | tf_op | source)
XLA Modules:
  0.0 408.3 jit_solution(1061171979769236281)
XLA Ops:
  7.2 0.8 convert_element_type.135
  8.1 0.8 fusion.48
  8.8 0.7 convert_element_type.126
  9.5 0.8 fusion.47
  10.3 6.3 %fusion.31 = f32[512,3072]{1,0:T(8,128)S(1)} fusion(bf16[1024,3072]{1,0:T(8,128)(2,1)} %param.23, bf16[1,512,1024]{2,1,0:T(8,128)(2,1)} %param.18, f32[1024]{0:T(1024)S(1)} %bitcast.111, f32[512]{0:T(512)S(1)} %bitcast.107, f32[1024]{0:T(1024)S(1)} %bitcast.109, f32[512]{0:T(512)S(1)} %broadcast_subtract_fusion), kind=kOutput, calls=%fused_computation.69 | convolution fusion | flops 3224371200 | bytes 13643776 | tf_op jit(solution)/shard_map/dot_general | solution.py:103
  16.6 1.2 slice.51
  17.7 1.9 fusion.16
  19.6 1.5 copy.38
  21.8 2.3 copy.39
  24.1 2.3 copy.40
  26.3 5.3 %fusion = (f32[16,512]{1,0:T(8,128)S(1)}, f32[16,512,512]{1,2,0:T(8,128)S(1)}) fusion(pred[512]{0:T(512)(128)(4,1)S(1)} %iota_compare_fusion.3, bf16[512,16,64]{0,2,1:T(8,128)(2,1)} %bitcast.98, bf16[512,16,64]{0,2,1:T(8,128)(2,1)} %bitcast.94), kind=kOutput, calls=%fused_computation.5 | convolution fusion | flops 549445632 | bytes 18907648 | tf_op jit(solution)/shard_map/while/body/eval_jaxpr/qhd,khd->hqk/dot_general | solution.py:39
  31.6 3.8 exponential_reduce_fusion
  35.5 1.8 copy-done.2
  37.3 3.9 fusion.1
  41.2 1.5 convolution_convert_fusion.1
  42.7 2.4 copy-done.3
  45.5 1.6 fusion.50
  47.7 0.6 copy-done.4
  48.4 1.4 fusion.27
  50.0 37.1 %all-gather.5.cloned.1.call-done = bf16[2048,1024]{1,0:T(8,128)(2,1)} async-done(((bf16[512,1024]{1,0:T(8,128)(2,1)}), bf16[2048,1024]{1,0:T(8,128)(2,1)}) %all-gather.5.cloned.1.call-update) | async-done | bytes 4194320 | tf_op jit(solution)/shard_map/all_gather | solution.py:127
  87.1 6.9 %fusion.23 = f32[4,512,1024]{2,1,0:T(8,128)S(1)} fusion(bf16[4,512,1024]{2,1,0:T(8,128)(2,1)} %bitcast.114, bf16[1024,1024]{1,0:T(8,128)(2,1)} %param.29), kind=kOutput, calls=%fused_computation.38 | convolution fusion | flops 4294967296 | bytes 14680064 | tf_op jit(solution)/shard_map/psd,df->psf/dot_general | solution.py:125
  94.0 3.2 copy-done.24
  97.2 6.5 %fusion.7 = f32[4,512,1024]{2,1,0:T(8,128)} fusion(f32[4,512,1024]{2,1,0:T(8,128)S(1)} %fusion.23, f32[1024]{0:T(1024)S(1)} %convert_element_type.138, bf16[1024,1024]{1,0:T(8,128)(2,1)S(1)} %copy-done), kind=kOutput, calls=%fused_computation.16 | convolution fusion | flops 4307550208 | bytes 18878464 | tf_op jit(solution)/shard_map/psf,fd->psd/dot_general | solution.py:136
  103.8 0.6 copy-done.17
  104.4 0.6 fusion.49
  105.0 1.3 fusion.40
  106.3 69.0 %reduce-scatter.3.cloned.1.call-done = f32[1,512,1024]{2,1,0:T(8,128)} async-done(((f32[4,512,1024]{2,1,0:T(8,128)}), f32[1,512,1024]{2,1,0:T(8,128)}) %reduce-scatter.3.cloned.1.call-update) | async-done | bytes 2097168 | tf_op jit(solution)/shard_map/reduce_scatter | solution.py:135
  175.3 2.9 fusion.45
  178.6 1.6 copy-done.7
  180.2 0.8 fusion.26
  181.1 1.8 convert_reduce_fusion.1
  182.9 34.6 %all-gather.7.cloned.1.call-done = bf16[2048,1024]{1,0:T(8,128)(2,1)} async-done(((bf16[512,1024]{1,0:T(8,128)(2,1)}), bf16[2048,1024]{1,0:T(8,128)(2,1)}) %all-gather.7.cloned.1.call-update) | async-done | bytes 4194320 | tf_op jit(solution)/shard_map/all_gather | solution.py:160
  217.5 10.3 %convert_reduce_fusion = (f32[1024]{0:T(1024)S(1)}, bf16[4,512,1024]{2,1,0:T(8,128)(2,1)S(1)}) fusion(f32[4,512,1024]{2,1,0:T(8,128)} %copy-done.24, f32[1024]{0:T(1024)S(1)} %convert_element_type.138, bf16[4,512,1024]{2,1,0:T(8,128)(2,1)} %bitcast.113, bf16[1024,1024]{1,0:T(8,128)(2,1)S(1)} %copy-done), kind=kOutput, calls=%fused_computation.13 | convolution fusion | flops 4322229248 | bytes 18882560 | tf_op jit(solution)/shard_map/psd,fd->psf/dot_general | solution.py:158
  227.9 6.9 %fusion.21 = f32[4,512,1024]{2,1,0:T(8,128)} fusion(bf16[4,512,1024]{2,1,0:T(8,128)(2,1)S(1)} %get-tuple-element.96, bf16[1024,1024]{1,0:T(8,128)(2,1)S(1)} %copy-done.20), kind=kOutput, calls=%fused_computation.36 | convolution fusion | flops 4294967296 | bytes 14680064 | tf_op jit(solution)/shard_map/psf,df->psd/dot_general | solution.py:169
  234.8 0.7 copy-done.18
  235.8 22.2 %psum.45 = f32[1024]{0:T(1024)} all-reduce(f32[1024]{0:T(1024)S(1)} %get-tuple-element.95), channel_id=1, replica_groups=mesh['dp'=8,'tensor'=4] {'dp'}, use_global_device_ids=true, to_apply=%region_21.22 | all-reduce | flops 1024 | bytes 8192 | tf_op jit(solution)/shard_map/psum | solution.py:166
  257.9 48.5 %reduce-scatter.5.cloned.1.call-done = f32[1,512,1024]{2,1,0:T(8,128)} async-done(((f32[4,512,1024]{2,1,0:T(8,128)}), f32[1,512,1024]{2,1,0:T(8,128)}) %reduce-scatter.5.cloned.1.call-update) | async-done | bytes 2097168 | tf_op jit(solution)/shard_map/reduce_scatter | solution.py:168
  306.4 4.2 %multiply_reduce_fusion.5 = (f32[512]{0:T(512)S(1)}, f32[512]{0:T(512)S(1)}, f32[1024]{0:T(1024)S(1)}, f32[512,1024]{1,0:T(8,128)S(1)}, bf16[1,512,1024]{2,1,0:T(8,128)(2,1)}) fusion(f32[1024]{0:T(1024)S(1)} %copy-done.13, f32[512]{0:T(512)S(1)} %add_rsqrt_fusion.1, f32[512,1024]{1,0:T(8,128)S(1)} %copy-done.5, f32[512]{0:T(512)S(1)} %broadcast_multiply_fusion.5, ...), kind=kLoop, calls=%fused_computation.64 | loop fusion | flops 10483712 | bytes 10520576 | tf_op jit(solution)/shard_map/reduce_sum | solution.py:33
  310.6 0.7 convert_reduce_fusion.2
  311.3 1.3 copy-done.12
  312.6 1.3 convolution_convert_fusion.2
  314.5 7.1 %convert_reduce_fusion.3 = (f32[16,64]{1,0:T(8,128)S(1)}, bf16[16,64,512]{2,1,0:T(8,128)(2,1)}) fusion(bf16[512,16,64]{0,2,1:T(8,128)(2,1)S(1)} %bitcast.96, bf16[16,512,512]{1,2,0:T(8,128)(2,1)} %copy-done.3), kind=kOutput, calls=%fused_computation.44 | convolution fusion | flops 538442752 | bytes 10489856 | tf_op jit(solution)/shard_map/while/body/eval_jaxpr/hqk,qhd->khd/dot_general | solution.py:66
  321.6 13.0 %multiply_reduce_fusion = (f32[16,512]{1,0:T(8,128)S(1)}, f32[16,512,512]{1,2,0:T(8,128)}) fusion(f32[16,512,512]{1,2,0:T(8,128)} %copy-done.2, f32[16,512]{1,0:T(8,128)S(1)} %log_add_fusion, pred[512]{0:T(512)(128)(4,1)S(1)} %iota_compare_fusion.3, bf16[512,16,64]{0,2,1:T(8,128)(2,1)S(1)} %bitcast.97, bf16[512,16,64]{0,2,1:T(8,128)(2,1)S(1)} %bitcast.93), kind=kOutput, calls=%fused_computation.1 | convolution fusion | flops 557834240 | bytes 35717632 | tf_op jit(solution)/shard_map/while/body/eval_jaxpr/qhd,khd->hqk/dot_general | solution.py:57
  334.5 12.6 %multiply_convert_fusion = bf16[16,512,512]{1,2,0:T(8,128)(2,1)S(1)} fusion(f32[16,512,512]{1,2,0:T(8,128)} %get-tuple-element.90, f32[16,512,512]{1,2,0:T(8,128)} %copy-done.2, f32[16,512]{1,0:T(8,128)S(1)} %get-tuple-element.89, f32[16,512]{1,0:T(8,128)S(1)} %log_add_fusion, pred[512]{0:T(512)(128)(4,1)S(1)} %iota_compare_fusion.3), kind=kLoop, calls=%fused_computation | loop fusion | flops 25165824 | bytes 42009088 | tf_op jit(solution)/shard_map/while/body/eval_jaxpr/convert_element_type | solution.py:59
  347.2 3.6 multiply_convert_fusion.3
  350.8 1.5 convert_reduce_fusion.4
  352.5 8.9 %add_bitcast_fusion = f32[1,512,1024]{2,1,0:T(8,128)} fusion(f32[512,1024]{1,0:T(8,128)} %copy-done.12, bf16[1024,3072]{1,0:T(8,128)(2,1)} %param.23, bf16[512,1024]{0,1:T(8,128)(2,1)} %bitcast.102, bf16[512,1024]{0,1:T(8,128)(2,1)} %bitcast.103, bf16[512,1024]{0,1:T(8,128)(2,1)S(1)} %bitcast.101), kind=kOutput, calls=%fused_computation.46 | convolution fusion | flops 3231186944 | bytes 13631488 | tf_op jit(solution)/shard_map/nc,dc->nd/dot_general | solution.py:190
  361.4 39.9 %all-reduce = (f32[2,1024]{1,0:T(2,128)}, f32[1024]{0:T(1024)}, f32[1024]{0:T(1024)}, f32[1024]{0:T(1024)}, f32[1024]{0:T(1024)}) all-reduce(f32[2,1024]{1,0:T(2,128)S(1)} %pad_maximum_fusion, f32[1024]{0:T(1024)S(1)} %get-tuple-element.71, f32[1024]{0:T(1024)S(1)} %get-tuple-element.51, ...), channel_id=1, replica_groups=mesh['dp'=8,'tensor'=4] {'dp','tensor'}, use_global_device_ids=true, to_apply=%region_15.16 | all-reduce | flops 6144 | bytes 49152 | tf_op jit(solution)/shard_map/psum | solution.py:199
  (71 shorter events, 2.9 us)
Async XLA Ops:
  7.2 90.1 %copy-start = (bf16[1024,1024]{1,0:T(8,128)(2,1)S(1)}, bf16[1024,1024]{1,0:T(8,128)(2,1)}, u32[]{:S(2)}) copy-start(bf16[1024,1024]{1,0:T(8,128)(2,1)} %param.31) | copy-start | bytes 6291460
  7.2 79.9 %all-gather.5.cloned.1.call-start = ((), (), s32[]{:S(2)}) async-start(), calls=%async_computation.4 | async-start | bytes 5242880 | tf_op jit(solution)/shard_map/all_gather | solution.py:127
  21.1 20.1 %copy-start.8 = (bf16[512,1024]{0,1:T(8,128)(2,1)}, bf16[512,1024]{0,1:T(8,128)(2,1)S(1)}, u32[]{:S(2)}) copy-start(bf16[512,1024]{0,1:T(8,128)(2,1)S(1)} %copy.38) | copy-start | bytes 3145732
  31.6 5.7 %copy-start.2 = (f32[16,512,512]{1,2,0:T(8,128)}, f32[16,512,512]{1,2,0:T(8,128)S(1)}, u32[]{:S(2)}) copy-start(f32[16,512,512]{1,2,0:T(8,128)S(1)} %get-tuple-element.86) | copy-start | bytes 50331652
  41.2 3.9 copy-start.3
  41.2 3.9 copy-start.21
  41.2 4.2 %copy-start.23 = (bf16[1,512,1024]{2,1,0:T(8,128)(2,1)S(1)}, bf16[1,512,1024]{2,1,0:T(8,128)(2,1)}, u32[]{:S(2)}) copy-start(bf16[1,512,1024]{2,1,0:T(8,128)(2,1)} %param.18) | copy-start | bytes 3145732
  47.0 1.3 copy-start.4
  47.0 0.7 copy-start.15
  47.0 1.3 copy-start.13
  48.4 1.6 copy-start.16
  49.8 125.5 %reduce-scatter.3.cloned.1.call-start = ((), (), s32[]{:S(2)}) async-start(), calls=%async_computation.2 | async-start | bytes 10485760 | tf_op jit(solution)/shard_map/reduce_scatter | solution.py:135
  94.0 3.2 copy-start.24
  103.7 0.7 copy-start.17
  103.7 0.7 copy-start.19
  103.7 113.8 %all-gather.7.cloned.1.call-start = ((), (), s32[]{:S(2)}) async-start(), calls=%async_computation.5 | async-start | bytes 5242880 | tf_op jit(solution)/shard_map/all_gather | solution.py:160
  178.2 2.8 copy-start.6
  178.2 2.0 copy-start.7
  178.3 2.0 copy-start.14
  182.9 123.5 %reduce-scatter.5.cloned.1.call-start = ((), (), s32[]{:S(2)}) async-start(), calls=%async_computation.3 | async-start | bytes 10485760 | tf_op jit(solution)/shard_map/reduce_scatter | solution.py:168
  217.5 10.3 %copy-start.20 = (bf16[1024,1024]{1,0:T(8,128)(2,1)S(1)}, bf16[1024,1024]{1,0:T(8,128)(2,1)}, u32[]{:S(2)}) copy-start(bf16[1024,1024]{1,0:T(8,128)(2,1)} %param.29) | copy-start | bytes 6291460
  234.8 0.7 copy-start.18
  234.8 71.6 %copy-start.5 = (f32[512,1024]{1,0:T(8,128)S(1)}, f32[512,1024]{1,0:T(8,128)}, u32[]{:S(2)}) copy-start(f32[512,1024]{1,0:T(8,128)} %copy-done.4) | copy-start | bytes 6291460
  310.6 2.0 copy-start.22
  311.3 1.3 copy-start.12
  314.5 7.1 %copy-start.9 = (bf16[512,1024]{0,1:T(8,128)(2,1)S(1)}, bf16[512,1024]{0,1:T(8,128)(2,1)}, u32[]{:S(2)}) copy-start(bf16[512,1024]{0,1:T(8,128)(2,1)} %copy-done.8) | copy-start | bytes 3145732
  334.5 12.6 %copy-start.11 = (bf16[512,1024]{0,1:T(8,128)(2,1)S(1)}, bf16[512,1024]{0,1:T(8,128)(2,1)}, u32[]{:S(2)}) copy-start(bf16[512,1024]{0,1:T(8,128)(2,1)} %copy.39) | copy-start | bytes 3145732
  347.2 3.6 copy-start.10
  352.5 48.8 %copy-start.1 = (bf16[1024,1024]{1,0:T(8,128)(2,1)S(1)}, bf16[1024,1024]{1,0:T(8,128)(2,1)}, u32[]{:S(2)}) copy-start(bf16[1024,1024]{1,0:T(8,128)(2,1)} %param.31) | copy-start | bytes 6291460
Sparse Core Ops, SparseCore 0:
  49.9 37.1 all-gather.4
  103.9 71.3 reduce-scatter.2
  183.0 34.4 all-gather.6
  234.9 71.3 reduce-scatter.4
where the time goes:
time: 416 us; the launch traced here: 408 us
  waiting for transfers between devices  189 us (45%)
  matrix products  80.6 us (19%)
  blocking collectives  62 us (15%)
  other arithmetic  37.9 us (9%)
  local copies, waits for them, and re-layouts  23 us (6%)
  between operations  15.2 us (4%)
    reduce_scatter x1, waiting for transfers between devices, local(): lax.psum_scatter(jnp.einsum('psf,fd->psd', rows, ffn_weight, preferred_el...  69 us
    reduce_scatter x1, waiting for transfers between devices, local(): lax.psum_scatter(jnp.einsum('psf,df->psd', rows, in_weight, preferred_ele...  48.5 us
    psum x1, blocking collectives, local(): lax.psum((grad_qv, grad_out_bias, grad_shift_one, grad_ffn_bias, grad_shi...  39.9 us
    all_gather x1, waiting for transfers between devices, local(): lax.all_gather(first_low.reshape(pairs, seq, width), 'tensor', axis=0, ti...  37.1 us
    all_gather x1, waiting for transfers between devices, local(): lax.all_gather(grad_ffn.reshape(pairs, seq, width), 'tensor', axis=0, til...  34.6 us
    psum x1, blocking collectives, local(): grad_in_bias = lax.psum(grad_in_part, 'dp')  22.2 us
    dot_general x1, matrix products, attend_backward(): jnp.einsum('qhd,khd->hqk', grad_mixed, value, preferred_element_type=jnp....  13 us
    unnamed x50, local copies, waits for them, and re-layouts  12.9 us
  transfers between devices with their start and end apart: 4, of which 4 were waited for; matrix products, arithmetic and copies ran while one was open for 1% of the time, Pallas kernels for 0%

commit v1 on v0

--- a/solution.py
+++ b/solution.py
@@ -100,6 +100,9 @@
     embedded = (tokens.astype(jnp.float32) + (1.0 - second) * table[0] + second * table[1]).reshape(
         flat, width
     )
+    in_full = lax.all_gather(in_weight, "tensor", axis=1, tiled=True)
+    ffn_full = lax.all_gather(ffn_weight, "tensor", axis=0, tiled=True)
+    bias_full = lax.all_gather(in_bias, "tensor", axis=0, tiled=True)
     packed = jnp.dot(embedded.astype(jnp.bfloat16), qkv_weight, preferred_element_type=jnp.float32)
     attn_bias = qv_bias.astype(jnp.float32)
     query = (packed[:, :width] + attn_bias[0]).astype(jnp.bfloat16)
@@ -120,24 +123,21 @@
         embedded + branch, gain_one, shift_one.astype(jnp.float32)
     )
     first_low = first.astype(jnp.bfloat16)
-    in_shift = in_bias.astype(jnp.float32)
+    in_shift = bias_full.astype(jnp.float32)
     inner = (
         jnp.einsum(
             "psd,df->psf",
-            lax.all_gather(first_low.reshape(pairs, seq, width), "tensor", axis=0, tiled=True),
-            in_weight,
+            first_low.reshape(pairs, seq, width),
+            in_full,
             preferred_element_type=jnp.float32,
         )
         + in_shift
     )
     hidden = gelu_erf(inner).astype(jnp.bfloat16)
     rows = hidden
-    outer = lax.psum_scatter(
-        jnp.einsum("psf,fd->psd", rows, ffn_weight, preferred_element_type=jnp.float32),
-        "tensor",
-        scatter_dimension=0,
-        tiled=True,
-    ).reshape(flat, width)
+    outer = jnp.einsum("psf,fd->psd", rows, ffn_full, preferred_element_type=jnp.float32).reshape(
+        flat, width
+    )
     final, normed_two, scale_two = norm_forward(
         first + outer + ffn_bias.astype(jnp.float32), gain_two, shift_two.astype(jnp.float32)
     )
@@ -157,19 +157,15 @@
     grad_ffn_bias = jnp.sum(grad_ffn.astype(jnp.float32), axis=0)
     back = jnp.einsum(
         "psd,fd->psf",
-        lax.all_gather(grad_ffn.reshape(pairs, seq, width), "tensor", axis=0, tiled=True),
-        ffn_weight,
+        grad_ffn.reshape(pairs, seq, width),
+        ffn_full,
         preferred_element_type=jnp.float32,
     )
     grad_inner = (back * gelu_slope(inner)).astype(jnp.bfloat16)
     grad_in_part = jnp.sum(grad_inner.astype(jnp.float32), axis=(0, 1))
-    grad_in_bias = lax.psum(grad_in_part, "dp")
     rows = grad_inner
-    grad_first = lax.psum_scatter(
-        jnp.einsum("psf,df->psd", rows, in_weight, preferred_element_type=jnp.float32),
-        "tensor",
-        scatter_dimension=0,
-        tiled=True,
+    grad_first = jnp.einsum(
+        "psf,df->psd", rows, in_full, preferred_element_type=jnp.float32
     ).reshape(flat, width)
     grad_first = grad_first + grad_second
     grad_shift_one = jnp.sum(grad_first, axis=0)
@@ -197,7 +193,12 @@
         ]
     )
     totals = lax.psum(
-        (grad_qv, grad_out_bias, grad_shift_one, grad_ffn_bias, grad_shift_two), ("dp", "tensor")
+        (grad_qv, grad_out_bias, grad_shift_one, grad_ffn_bias, grad_shift_two, grad_in_part),
+        ("dp", "tensor"),
+    )
+    units = in_bias.shape[0]
+    grad_in_bias = lax.dynamic_slice_in_dim(
+        totals[5], lax.axis_index("tensor") * units, units, axis=0
     )
     return (
         activations,

time: 416 us -> 270 us (0.65)
  waiting for transfers between devices: 189 us -> 63.7 us
  blocking collectives: 62 us -> 47.7 us
  matrix products: 80.6 us -> 93.7 us
  other arithmetic: 37.9 us -> 29 us
  local copies, waits for them, and re-layouts: 23 us -> 16.6 us
    reduce_scatter x2 -> x0, waiting for transfers between devices: 117 us -> none  [the longest x1 69 us: local(): lax.psum_scatter(jnp.einsum('psf,fd->psd', rows, ffn_weight, preferred_el...]
    psum x1 -> x0, blocking collectives: 22.2 us -> none  [local(): grad_in_bias = lax.psum(grad_in_part, 'dp')]
    dot_general x4, matrix products: 30.6 us -> 42.6 us  [the longest x1 13.1 us: local(): jnp.einsum('psd,df->psf', first_low.reshape(pairs, seq, width), in_full,...]
    all_gather x2, waiting for transfers between devices: 71.7 us -> 62.4 us  [the longest x1 46.8 us: local(): ffn_full = lax.all_gather(ffn_weight, 'tensor', axis=0, tiled=True)]
    all_gather x0 -> x1, blocking collectives: none -> 6.89 us  [local(): bias_full = lax.all_gather(in_bias, 'tensor', axis=0, tiled=True)]
    unnamed x50, local copies, waits for them, and re-layouts: 12.9 us -> 7.6 us
    reduce_sum x2 -> x1, other arithmetic: 5.05 us -> 0.84 us  [norm_backward(): centered = scaled - jnp.mean(scaled, axis=-1, keepdims=True)]
  transfers between devices with their start and end apart: 4 -> 2, of which waited for: 4 -> 2; matrix products, arithmetic and copies ran while one was open for 1% -> 17% of each run, Pallas kernels for 0% -> 0%
where the time goes in v1:
time: 270 us; the launch traced here: 266 us
  matrix products  93.7 us (35%)
  waiting for transfers between devices  63.7 us (24%)
  blocking collectives  47.7 us (18%)
  other arithmetic  29 us (11%)
  local copies, waits for them, and re-layouts  16.6 us (6%)
  between operations  15.4 us (6%)
    all_gather x1, waiting for transfers between devices, local(): ffn_full = lax.all_gather(ffn_weight, 'tensor', axis=0, tiled=True)  46.8 us
    psum x1, blocking collectives, local(): lax.psum((grad_qv, grad_out_bias, grad_shift_one, grad_ffn_bias, grad_shi...  40.8 us
    all_gather x1, waiting for transfers between devices, local(): in_full = lax.all_gather(in_weight, 'tensor', axis=1, tiled=True)  15.6 us
    dot_general x1, matrix products, attend_backward(): jnp.einsum('qhd,khd->hqk', grad_mixed, value, preferred_element_type=jnp....  13.5 us
    dot_general x1, matrix products, local(): jnp.einsum('psd,df->psf', first_low.reshape(pairs, seq, width), in_full,...  13.1 us
    convert_element_type x1, other arithmetic, attend_backward(): grad_scores = (probs * (grad_probs - inner_sum)).astype(jnp.bfloat16)  12.4 us
    dot_general x1, matrix products, local(): jnp.einsum('psd,fd->psf', grad_ffn.reshape(pairs, seq, width), ffn_full,...  12.3 us
    dot_general x1, matrix products, local(): jnp.einsum('psf,fd->psd', rows, ffn_full, preferred_element_type=jnp.floa...  10.2 us
  transfers between devices with their start and end apart: 2, of which 2 were waited for; matrix products, arithmetic and copies ran while one was open for 17% of the time, Pallas kernels for 0%

profile of v1, /device:TPU:0, one launch (start us, length us, event | category | flops | bytes accessed | tf_op | source)
XLA Modules:
  0.0 266.3 jit_solution(15663924303456042487)
XLA Ops:
  7.2 0.0 all-gather.3.cloned.1.call-start
  7.3 0.7 all-gather.3.cloned.1.call-update
  7.9 0.0 all-gather.5.cloned.1.call-start
  8.0 0.7 all-gather.5.cloned.1.call-update
  8.8 6.0 %fusion.26 = f32[512,3072]{1,0:T(8,128)S(1)} fusion(bf16[1024,3072]{1,0:T(8,128)(2,1)} %param.23, bf16[1,512,1024]{2,1,0:T(8,128)(2,1)S(1)} %copy-done.21, f32[1024]{0:T(1024)S(1)} %bitcast.86, f32[512]{0:T(512)S(1)} %bitcast.82, f32[1024]{0:T(1024)S(1)} %bitcast.84, f32[512]{0:T(512)S(1)} %broadcast_subtract_fusion), kind=kOutput, calls=%fused_computation.63 | convolution fusion | flops 3224371200 | bytes 13643776 | tf_op jit(solution)/shard_map/dot_general | solution.py:106
  14.8 0.2 slice.51
  15.0 0.5 copy-done.12
  15.5 1.9 fusion.16
  17.4 2.4 copy.47
  19.8 1.3 copy.48
  21.8 1.6 copy.46
  23.4 6.9 %all_gather.10 = bf16[4096]{0:T(1024)(128)(2,1)S(1)} all-gather(bf16[1024]{0:T(1024)(128)(2,1)S(1)} %copy-done.16), channel_id=1, replica_groups=mesh['dp'=8,'tensor'=4] {'tensor'}, dimensions={0}, use_global_device_ids=true | all-gather | bytes 10240 | tf_op jit(solution)/shard_map/all_gather | solution.py:105
  30.3 0.6 fusion.45
  30.9 1.3 fusion.40
  32.2 1.5 fusion.18
  33.7 5.3 %fusion = (f32[16,512]{1,0:T(8,128)S(1)}, f32[16,512,512]{1,2,0:T(8,128)S(1)}) fusion(pred[512]{0:T(512)(128)(4,1)S(1)} %iota_compare_fusion.3, bf16[512,16,64]{0,2,1:T(8,128)(2,1)} %bitcast.73, bf16[512,16,64]{0,2,1:T(8,128)(2,1)} %bitcast.69), kind=kOutput, calls=%fused_computation.5 | convolution fusion | flops 549445632 | bytes 18907648 | tf_op jit(solution)/shard_map/while/body/eval_jaxpr/qhd,khd->hqk/dot_general | solution.py:39
  39.0 3.8 %exponential_reduce_fusion = f32[16,512]{1,0:T(8,128)S(1)} fusion(f32[16,512,512]{1,2,0:T(8,128)S(1)} %get-tuple-element.84, f32[16,512]{1,0:T(8,128)S(1)} %get-tuple-element.83, pred[512]{0:T(512)(128)(4,1)S(1)} %iota_compare_fusion.3), kind=kLoop, calls=%fused_computation.3 | loop fusion | flops 16769024 | bytes 16843264 | tf_op jit(solution)/shard_map/while/body/eval_jaxpr/reduce_sum | solution.py:47
  42.9 1.8 copy-done.1
  44.7 3.9 %fusion.1 = bf16[16,512,512]{1,2,0:T(8,128)(2,1)S(1)} fusion(f32[16,512,512]{1,2,0:T(8,128)S(1)} %get-tuple-element.84, f32[16,512]{1,0:T(8,128)S(1)} %log_add_fusion, pred[512]{0:T(512)(128)(4,1)S(1)} %iota_compare_fusion.3), kind=kLoop, calls=%fused_computation.7 | loop fusion | flops 16777216 | bytes 25199104 | tf_op jit(solution)/shard_map/while/body/eval_jaxpr/convert_element_type | solution.py:48
  48.6 1.5 convolution_convert_fusion.1
  50.1 1.7 copy-done.2
  51.8 1.6 fusion.46
  53.4 1.3 copy-done.7
  54.7 0.3 multiply_reduce_fusion.4
  55.1 15.6 %all-gather.3.cloned.1.call-done = bf16[1024,4096]{1,0:T(8,128)(2,1)} async-done(((bf16[1024,1024]{1,0:T(8,128)(2,1)}), bf16[1024,4096]{1,0:T(8,128)(2,1)}) %all-gather.3.cloned.1.call-update) | async-done | bytes 8388624 | tf_op jit(solution)/shard_map/all_gather | solution.py:103
  70.7 13.1 %fusion.23 = f32[512,4096]{1,0:T(8,128)} fusion(bf16[1024,4096]{1,0:T(8,128)(2,1)} %all-gather.3.cloned.1.call-done, f32[512,1024]{1,0:T(8,128)} %copy-done.7, f32[1024]{0:T(1024)S(1)} %convert_element_type.139, f32[1024]{0:T(1024)S(1)} %copy-done.13, f32[512]{0:T(512)S(1)} %add_rsqrt_fusion.1, f32[512]{0:T(512)S(1)} %broadcast_multiply_fusion.5), kind=kOutput, calls=%fused_computation.61 | convolution fusion | flops 4297588736 | bytes 18886656 | tf_op jit(solution)/shard_map/psd,df->psf/dot_general | solution.py:128
  83.7 46.8 %all-gather.5.cloned.1.call-done = bf16[4096,1024]{1,0:T(8,128)(2,1)} async-done(((bf16[1024,1024]{1,0:T(8,128)(2,1)}), bf16[4096,1024]{1,0:T(8,128)(2,1)}) %all-gather.5.cloned.1.call-update) | async-done | bytes 8388624 | tf_op jit(solution)/shard_map/all_gather | solution.py:104
  130.5 10.2 %fusion.47 = (f32[512]{0:T(512)S(1)}, f32[512,1024]{1,0:T(8,128)S(1)}) fusion(f32[1024]{0:T(1024)S(1)} %convert_element_type.143, bf16[4096,1024]{1,0:T(8,128)(2,1)} %all-gather.5.cloned.1.call-done, f32[512,4096]{1,0:T(8,128)} %fusion.23, f32[4096]{0:T(1024)S(1)} %convert_element_type.141, f32[1024]{0:T(1024)S(1)} %convert_element_type.139, ...), kind=kOutput, calls=%fused_computation.99 | convolution fusion | flops 4311219712 | bytes 21006336 | tf_op jit(solution)/shard_map/psf,fd->psd/dot_general | solution.py:138
  140.7 0.3 multiply_reduce_fusion.3
  141.1 0.8 copy-done.5
  141.9 0.8 fusion.19
  142.8 1.9 convert_reduce_fusion.1
  144.7 12.3 %convert_reduce_fusion = (f32[4096]{0:T(1024)S(1)}, bf16[512,4096]{1,0:T(8,128)(2,1)}) fusion(f32[512,4096]{1,0:T(8,128)} %fusion.23, f32[4096]{0:T(1024)S(1)} %convert_element_type.141, bf16[4096,1024]{1,0:T(8,128)(2,1)} %all-gather.5.cloned.1.call-done, f32[512,1024]{1,0:T(8,128)S(1)} %get-tuple-element.71), kind=kOutput, calls=%fused_computation.13 | convolution fusion | flops 4322750464 | bytes 23101440 | tf_op jit(solution)/shard_map/psd,fd->psf/dot_general | solution.py:158
  157.0 7.0 %multiply_reduce_fusion.5 = (f32[512]{0:T(512)S(1)}, f32[512]{0:T(512)S(1)}, f32[1024]{0:T(1024)S(1)}, f32[512,1024]{1,0:T(8,128)S(1)}) fusion(f32[1024]{0:T(1024)S(1)} %copy-done.13, f32[512]{0:T(512)S(1)} %add_rsqrt_fusion.1, f32[512,1024]{1,0:T(8,128)S(1)} %copy-done.8, f32[512]{0:T(512)S(1)} %broadcast_multiply_fusion.5, ...), kind=kOutput, calls=%fused_computation.56 | convolution fusion | flops 4299159552 | bytes 18890752 | tf_op jit(solution)/shard_map/psf,df->psd/dot_general | solution.py:167
  164.1 0.7 convert_reduce_fusion.2
  164.8 1.3 copy-done.9
  166.1 2.3 convolution_convert_fusion.2
  168.4 2.3 copy.50
  170.7 13.5 %multiply_reduce_fusion = (f32[16,512]{1,0:T(8,128)S(1)}, f32[16,512,512]{1,2,0:T(8,128)}) fusion(f32[16,512,512]{1,2,0:T(8,128)} %copy-done.1, f32[16,512]{1,0:T(8,128)S(1)} %log_add_fusion, pred[512]{0:T(512)(128)(4,1)S(1)} %iota_compare_fusion.3, bf16[512,16,64]{0,2,1:T(8,128)(2,1)} %bitcast.71, bf16[512,16,64]{0,2,1:T(8,128)(2,1)S(1)} %bitcast.68), kind=kOutput, calls=%fused_computation.1 | convolution fusion | flops 557834240 | bytes 35717632 | tf_op jit(solution)/shard_map/while/body/eval_jaxpr/qhd,khd->hqk/dot_general | solution.py:57
  184.2 7.0 %convert_reduce_fusion.3 = (f32[16,64]{1,0:T(8,128)S(1)}, bf16[16,64,512]{2,1,0:T(8,128)(2,1)}) fusion(bf16[512,16,64]{0,2,1:T(8,128)(2,1)S(1)} %bitcast.72, bf16[16,512,512]{1,2,0:T(8,128)(2,1)} %copy-done.2), kind=kOutput, calls=%fused_computation.35 | convolution fusion | flops 538442752 | bytes 10489856 | tf_op jit(solution)/shard_map/while/body/eval_jaxpr/hqk,qhd->khd/dot_general | solution.py:66
  191.3 12.4 %multiply_convert_fusion = bf16[16,512,512]{1,2,0:T(8,128)(2,1)S(1)} fusion(f32[16,512,512]{1,2,0:T(8,128)} %get-tuple-element.91, f32[16,512,512]{1,2,0:T(8,128)} %copy-done.1, f32[16,512]{1,0:T(8,128)S(1)} %get-tuple-element.90, f32[16,512]{1,0:T(8,128)S(1)} %log_add_fusion, pred[512]{0:T(512)(128)(4,1)S(1)} %iota_compare_fusion.3), kind=kLoop, calls=%fused_computation | loop fusion | flops 25165824 | bytes 42009088 | tf_op jit(solution)/shard_map/while/body/eval_jaxpr/convert_element_type | solution.py:59
  203.7 1.5 convert_reduce_fusion.4
  205.2 3.6 %multiply_convert_fusion.3 = bf16[16,64,512]{2,1,0:T(8,128)(2,1)} fusion(bf16[512,16,64]{0,2,1:T(8,128)(2,1)S(1)} %bitcast.74, bf16[16,512,512]{1,2,0:T(8,128)(2,1)S(1)} %multiply_convert_fusion), kind=kOutput, calls=%fused_computation.38 | convolution fusion | flops 537919488 | bytes 10485760 | tf_op jit(solution)/shard_map/while/body/eval_jaxpr/hqk,qhd->khd/dot_general | solution.py:63
  208.8 0.1 stack.9
  208.9 0.1 stack.10
  208.9 40.8 %all-reduce = (f32[2,1024]{1,0:T(2,128)}, f32[1024]{0:T(1024)}, f32[1024]{0:T(1024)}, f32[4096]{0:T(1024)S(1)}, f32[1024]{0:T(1024)}, /*index=5*/f32[1024]{0:T(1024)}) all-reduce(f32[2,1024]{1,0:T(2,128)S(1)} %pad_maximum_fusion, f32[1024]{0:T(1024)S(1)} %get-tuple-element.72, ...), channel_id=1, replica_groups=mesh['dp'=8,'tensor'=4] {'dp','tensor'}, use_global_device_ids=true, to_apply=%region_13.14 | all-reduce | flops 10240 | bytes 81920 | tf_op jit(solution)/shard_map/psum | solution.py:195
  249.7 0.6 dynamic_slice.26
  250.3 8.8 %add_bitcast_fusion = f32[1,512,1024]{2,1,0:T(8,128)} fusion(f32[512,1024]{1,0:T(8,128)} %copy-done.9, bf16[1024,3072]{1,0:T(8,128)(2,1)} %param.23, bf16[512,1024]{0,1:T(8,128)(2,1)} %bitcast.77, bf16[512,1024]{0,1:T(8,128)(2,1)} %bitcast.78, bf16[512,1024]{0,1:T(8,128)(2,1)S(1)} %bitcast.76), kind=kOutput, calls=%fused_computation.37 | convolution fusion | flops 3231186944 | bytes 13631488 | tf_op jit(solution)/shard_map/nc,dc->nd/dot_general | solution.py:186
  (64 shorter events, 0.2 us)
Async XLA Ops:
  7.2 44.6 %copy-start = (bf16[1024,1024]{1,0:T(8,128)(2,1)S(1)}, bf16[1024,1024]{1,0:T(8,128)(2,1)}, u32[]{:S(2)}) copy-start(bf16[1024,1024]{1,0:T(8,128)(2,1)} %param.25) | copy-start | bytes 6291460
  7.2 1.5 copy-start.19
  7.2 1.5 copy-start.11
  7.2 1.6 copy-start.21
  7.2 63.4 %all-gather.3.cloned.1.call-start = ((), (), s32[]{:S(2)}) async-start(), calls=%async_computation | async-start | bytes 10485760 | tf_op jit(solution)/shard_map/all_gather | solution.py:103
  7.9 122.6 %all-gather.5.cloned.1.call-start = ((), (), s32[]{:S(2)}) async-start(), calls=%async_computation.1 | async-start | bytes 10485760 | tf_op jit(solution)/shard_map/all_gather | solution.py:104
  14.8 0.7 copy-start.12
  19.7 3.6 %copy-start.14 = (bf16[1024]{0:T(1024)(128)(2,1)S(1)}, bf16[1024]{0:T(1024)(128)(2,1)}, u32[]{:S(2)}) copy-start(bf16[1024]{0:T(1024)(128)(2,1)} %param.26) | copy-start | bytes 6148
  19.7 3.6 %copy-start.15 = (bf16[1024]{0:T(1024)(128)(2,1)S(1)}, bf16[1024]{0:T(1024)(128)(2,1)}, u32[]{:S(2)}) copy-start(bf16[1024]{0:T(1024)(128)(2,1)} %param.28) | copy-start | bytes 6148
  19.7 3.6 %copy-start.16 = (bf16[1024]{0:T(1024)(128)(2,1)S(1)}, bf16[1024]{0:T(1024)(128)(2,1)}, u32[]{:S(2)}) copy-start(bf16[1024]{0:T(1024)(128)(2,1)} %param.30) | copy-start | bytes 6148
  19.7 10.5 %copy-start.17 = (bf16[1024]{0:T(1024)(128)(2,1)S(1)}, bf16[1024]{0:T(1024)(128)(2,1)}, u32[]{:S(2)}) copy-start(bf16[1024]{0:T(1024)(128)(2,1)} %param.32) | copy-start | bytes 6148
  19.8 10.5 %copy-start.18 = (bf16[1024]{0:T(1024)(128)(2,1)S(1)}, bf16[1024]{0:T(1024)(128)(2,1)}, u32[]{:S(2)}) copy-start(bf16[1024]{0:T(1024)(128)(2,1)} %param.34) | copy-start | bytes 6148
  19.8 10.5 %copy-start.20 = (s32[1,2]{1,0:T(1,128)S(1)}, s32[1,2]{1,0:T(1,128)}, u32[]{:S(2)}) copy-start(s32[1,2]{1,0:T(1,128)} %param.20) | copy-start | bytes 28
  39.0 5.7 %copy-start.1 = (f32[16,512,512]{1,2,0:T(8,128)}, f32[16,512,512]{1,2,0:T(8,128)S(1)}, u32[]{:S(2)}) copy-start(f32[16,512,512]{1,2,0:T(8,128)S(1)} %get-tuple-element.84) | copy-start | bytes 50331652
  48.6 3.2 %copy-start.2 = (bf16[16,512,512]{1,2,0:T(8,128)(2,1)}, bf16[16,512,512]{1,2,0:T(8,128)(2,1)S(1)}, u32[]{:S(2)}) copy-start(bf16[16,512,512]{1,2,0:T(8,128)(2,1)S(1)} %fusion.1) | copy-start | bytes 25165828
  48.6 3.2 %copy-start.22 = (bf16[1,512,1024]{2,1,0:T(8,128)(2,1)S(1)}, bf16[1,512,1024]{2,1,0:T(8,128)(2,1)}, u32[]{:S(2)}) copy-start(bf16[1,512,1024]{2,1,0:T(8,128)(2,1)} %param.18) | copy-start | bytes 3145732
  53.4 1.3 copy-start.7
  53.4 17.3 %copy-start.13 = (f32[1024]{0:T(1024)S(1)}, f32[1024]{0:T(1024)}, u32[]{:S(2)}) copy-start(f32[1024]{0:T(1024)} %param.27) | copy-start | bytes 12292
  140.7 1.2 copy-start.5
  140.7 1.2 copy-start.10
  142.8 14.2 %slice-start = ((s8[8388608]{0:T(1024)(128)(4,1)}), s8[4194304]{0:T(1024)(128)(4,1)S(1)}, s32[]{:S(2)}) async-start(s8[8388608]{0:T(1024)(128)(4,1)} %bitcast.88), calls=%async_computation.2 | async-start | bytes 8388608
  144.7 12.3 %copy-start.8 = (f32[512,1024]{1,0:T(8,128)S(1)}, f32[512,1024]{1,0:T(8,128)}, u32[]{:S(2)}) copy-start(f32[512,1024]{1,0:T(8,128)} %copy-done.7) | copy-start | bytes 6291460
  144.7 12.3 %slice-start.1 = ((s8[8388608]{0:T(1024)(128)(4,1)}), s8[4194304]{0:T(1024)(128)(4,1)S(1)}, s32[]{:S(2)}) async-start(s8[8388608]{0:T(1024)(128)(4,1)} %bitcast.88), calls=%async_computation.3 | async-start | bytes 8388608
  164.8 1.3 copy-start.9
  170.7 13.5 %copy-start.4 = (bf16[512,1024]{0,1:T(8,128)(2,1)S(1)}, bf16[512,1024]{0,1:T(8,128)(2,1)}, u32[]{:S(2)}) copy-start(bf16[512,1024]{0,1:T(8,128)(2,1)} %copy.50) | copy-start | bytes 3145732
  191.2 12.4 %copy-start.3 = (bf16[512,1024]{0,1:T(8,128)(2,1)S(1)}, bf16[512,1024]{0,1:T(8,128)(2,1)}, u32[]{:S(2)}) copy-start(bf16[512,1024]{0,1:T(8,128)(2,1)} %copy.48) | copy-start | bytes 3145732
  203.6 1.5 copy-start.6
Sparse Core Ops, SparseCore 0:
  9.6 61.0 all-gather.2
  72.2 58.2 all-gather.4

commit v2 on v0

v2 whole, which is shorter than its diff:
```python
import functools

import jax
import jax.numpy as jnp
from jax import lax
from jax.experimental import pallas as pl
from jax.experimental.pallas import tpu as pltpu
from jax.sharding import PartitionSpec as P

HEADS = 16
TILE = 256
LANES = 128
BLOCK = 64
F32 = jnp.float32
BF16 = jnp.bfloat16
MESH = pl.DeviceIdType.MESH
NT = (((1,), (1,)), ((), ()))
root_half = 0.7071067811865476
inv_root_tau = 0.3989422804014327
eps_norm = 1e-06
STOP = 99


def dot(a, b):
    return jnp.dot(a, b, preferred_element_type=F32)


def dot_nt(a, b):
    return lax.dot_general(a, b, NT, preferred_element_type=F32)


def mean_rows(value):
    return jnp.sum(value, axis=-1, keepdims=True) * (1.0 / value.shape[-1])


def cols(n, size=TILE):
    return pl.ds(pl.multiple_of(n * size, size), size)


def fold8(value):
    return jnp.sum(value.reshape(value.shape[0] // 8, 8, value.shape[1]), axis=0)


def total8(value):
    return jnp.sum(value, axis=0, keepdims=True)


def flip(index, bit):
    return index + bit * (1 - 2 * (index // bit % 2))


def kernel(
    ranks, group,
    lengths, separators, small, in_b, tokens, cot, qkv_w, out_w, in_w, ffn_w,
    act_out, grad_out, qv_out, outb_out, shift1_out, inb_out, ffnb_out, shift2_out,
    qkvw, outw, inw, ffw, inb, q, k, v, pt, slope, hid, a0, a1, f0, f1, f2, tok, cotb, act, sc1, cs, csqv,
    ginb, rinb, ibuf, irec, tsum, sbuf, srec, tqv, qbuf, qrec,
    wsem, lsem, send, recv,
):
    rows, width = tok.shape
    tiles = width // TILE
    hd = width // HEADS
    chunks = inw.shape[0]
    units = in_w.shape[1]
    part = units // 4
    line = group // 2
    brow = units // LANES
    prow = part // LANES
    per = units // TILE
    length = lengths[0]
    sep0, sep1 = separators[0, 0], separators[0, 1]
    dp, tensor = lax.axis_index("dp"), lax.axis_index("tensor")
    y, core = tensor // 2, tensor % 2
    bits = [1 << b for b in range(ranks.bit_length() - 1)]

    def place(d, other):
        return (dp, (y + d + line) % line * 2 + (core + other) % 2)

    def rank(bit):
        return (flip(dp, bit), tensor)

    barrier = pltpu.get_barrier_semaphore()
    friends = [place(s // 2, s % 2) for s in range(1, group)] + [rank(b) for b in bits]
    for f in friends:
        pl.semaphore_signal(barrier, inc=1, device_id=f, device_id_type=MESH)

    count = [0]

    def remote(src, dst, device):
        i = count[0]
        count[0] += 1
        return pltpu.make_async_remote_copy(
            src_ref=src, dst_ref=dst, send_sem=send.at[i], recv_sem=recv.at[i], device_id=device, device_id_type=MESH
        )

    def natural(p):
        return (p + dp) % 2 + (p // 2 + dp // 2) % 2 * 2

    def piece(slot, p, i):
        u = slot * units + p * part
        if i < 2:
            return inw.at[u // TILE, pl.ds(i * width // 2, width // 2), pl.ds(u % TILE, part)]
        return ffw.at[pl.ds(u + (i - 2) * part // 2, part // 2), :]

    def source(p, i):
        u = pl.multiple_of(natural(p) * part, part)
        if i < 2:
            return in_w.at[pl.ds(i * width // 2, width // 2), pl.ds(u, part)]
        return ffn_w.at[pl.ds(u + (i - 2) * part // 2, part // 2), :]

    def load(i, src, dst):
        c = pltpu.make_async_copy(src, dst, lsem.at[i])
        c.start()
        return c

    c_tok = load(0, tokens, tok)
    c_qkv = []
    for n in range(3 * tiles):
        c = pltpu.make_async_copy(qkv_w.at[:, n * TILE : (n + 1) * TILE], qkvw.at[n], wsem.at[n])
        c.start()
        c_qkv.append(c)
    c_in = []
    for n in range(per):
        c = pltpu.make_async_copy(in_w.at[:, n * TILE : (n + 1) * TILE], inw.at[n], wsem.at[3 * tiles + n])
        c.start()
        c_in.append(c)
    c_out = load(1, out_w, outw)
    c_ffn = load(2, ffn_w, ffw.at[pl.ds(0, units), :])
    c_b = load(3, in_b, inb.at[pl.ds(0, brow)])
    c_cot = load(4, cot, cotb)

    far = range(1, line)
    direct = {d: [remote(source(p, i), piece(2 * d, p, i), place(-d, 0)) for p, i in ((0, 0), (0, 1), (0, 2), (0, 3), (3, 2), (3, 3))] for d in far}
    to_x = {d: [remote(piece(2 * d, p, i), piece(2 * d, p + 1, i), rank(1)) for p, i in ((0, 0), (0, 1), (0, 2), (0, 3), (2, 0))] for d in far}
    to_z = {d: [remote(piece(2 * d, p, i), piece(2 * d, p + 2, i), rank(2)) for p, i in ((0, 0), (0, 1), (0, 2), (0, 3), (1, 1))] for d in far}
    pass_on = {d: {(p, i): remote(piece(2 * d, p, i), piece(2 * d + 1, p, i), place(0, 1)) for p in range(4) for i in range(4)} for d in far}
    core_in = [remote(in_w.at[:, n * TILE : (n + 1) * TILE], inw.at[per + n], place(0, 1)) for n in range(per)]
    core_ffn = remote(ffn_w, ffw.at[pl.ds(units, units), :], place(0, 1))
    bias = [remote(in_b, inb.at[pl.ds(s * brow, brow)], place(-(s // 2), s % 2)) for s in range(1, group)]

    def relay(step):
        for d in far:
            yd, xd, zd, on = direct[d], to_x[d], to_z[d], pass_on[d]
            if step < 4:
                yd[step].wait_recv()
                xd[step].start()
                zd[step].start()
                on[0, step].start()
            if step == 1:
                zd[0].wait_recv()
                xd[4].start()
                on[2, 0].start()
                xd[0].wait_recv()
                on[1, 0].start()
            if step == 2:
                xd[1].wait_recv()
                zd[4].start()
                on[1, 1].start()
                zd[1].wait_recv()
                on[2, 1].start()
            if step == 3:
                xd[4].wait_recv()
                on[3, 0].start()
                zd[4].wait_recv()
                on[3, 1].start()
            if step >= 4:
                yd[step].wait_recv()
                on[3, step - 2].start()
                xd[step - 2].wait_recv()
                on[1, step - 2].start()
                zd[step - 2].wait_recv()
                on[2, step - 2].start()

    c_tok.wait()

    @pl.loop(0, rows // BLOCK)
    def _(i):
        r = cols(i, BLOCK)
        pos = lax.broadcasted_iota(jnp.int32, (BLOCK, width), 0) + i * BLOCK
        second = (pos > sep0) & (pos < length)
        e = tok[r, :].astype(F32) + jnp.where(second, small[1:2, :], small[0:1, :])
        f0[r, :] = e
        a0[r, :] = e.astype(BF16)

    pl.semaphore_wait(barrier, len(friends))
    for d in far:
        for c in direct[d]:
            c.start()
    for c in core_in + [core_ffn] + bias:
        c.start()

    for c in c_qkv:
        c.wait()

    @pl.loop(0, tiles)
    def _(n):
        q[n] = (dot(a0[...], qkvw[n]) + small[2:3, cols(n)]).astype(BF16) * jnp.asarray(hd**-0.5, BF16)

    @pl.loop(0, tiles)
    def _(n):
        k[n] = dot(a0[...], qkvw[n + tiles]).astype(BF16)

    @pl.loop(0, tiles)
    def _(n):
        v[n] = (dot(a0[...], qkvw[n + 2 * tiles]) + small[3:4, cols(n)]).astype(BF16)

    relay(0)

    low_half = lax.broadcasted_iota(jnp.int32, (rows, LANES), 1) < hd
    zero = jnp.zeros((rows, LANES), BF16)
    heads = TILE // hd

    def halves(pair):
        return jnp.where(low_half, pair, zero), jnp.where(low_half, zero, pair)

    @pl.loop(0, tiles)
    def _(n):
        vt = v[n].T
        outs = []
        for p in range(TILE // LANES):
            k2 = k[n, :, p * LANES : (p + 1) * LANES]
            for e, qm in enumerate(halves(q[n, :, p * LANES : (p + 1) * LANES])):
                h = 2 * p + e
                s = dot_nt(k2, qm)
                kpos = lax.broadcasted_iota(jnp.int32, s.shape, 0)
                s = jnp.where(kpos < length, s, -1e30)
                top = jnp.max(s, axis=0, keepdims=True)
                ex = jnp.exp(s - top)
                prob = (ex * (1.0 / jnp.sum(ex, axis=0, keepdims=True))).astype(BF16)
                pt[n * heads + h] = prob
                outs.append(dot(vt[h * hd : (h + 1) * hd], prob))
        a1[:, cols(n)] = jnp.concatenate(outs, axis=0).astype(BF16).T

        @pl.when(n == tiles // 2)
        def _():
            relay(1)

    c_out.wait()

    @pl.loop(0, tiles)
    def _(n):
        f1[:, cols(n)] = dot(a1[...], outw[:, cols(n)]) + small[4:5, cols(n)] + f0[:, cols(n)]

    @pl.loop(0, rows // BLOCK)
    def _(i):
        r = cols(i, BLOCK)
        x = f1[r, :]
        x = x - mean_rows(x)
        scale = lax.rsqrt(mean_rows(x * x) + eps_norm)
        normed = x * scale
        f0[r, :] = normed
        a0[r, :] = (normed * small[5:6, :] + small[6:7, :]).astype(BF16)
        sc1[r, :] = jnp.broadcast_to(scale, (BLOCK, LANES))

    relay(2)

    def hidden_units(c, first, second):
        x = dot(a0[...], inw[c]) + jnp.concatenate([inb[first], inb[second]], axis=1)
        cdf = 0.5 * (1.0 + lax.erf(x * root_half))
        hid[c] = (x * cdf).astype(BF16)
        slope[c] = cdf + x * (inv_root_tau * jnp.exp(-0.5 * x * x))

    for c in c_in + [c_b]:
        c.wait()
    for c in core_in + bias:
        c.wait_recv()

    @pl.loop(0, 2 * per)
    def _(c):
        hidden_units(c, 2 * c, 2 * c + 1)

    relay(3)
    for d in far:
        for p in range(4):
            pass_on[d][p, 0].wait_recv()
            pass_on[d][p, 1].wait_recv()

    def shuffled(r):
        return r // brow * brow + natural(r % brow // prow) * prow + r % prow

    @pl.loop(2 * per, chunks)
    def _(c):
        hidden_units(c, shuffled(2 * c), shuffled(2 * c + 1))

    relay(4)
    c_ffn.wait()
    core_ffn.wait_recv()

    @pl.loop(0, tiles)
    def _(t):
        acc = dot(hid[0], ffw[0:TILE, cols(t)])
        for c in range(1, 2 * per):
            acc += dot(hid[c], ffw[c * TILE : (c + 1) * TILE, cols(t)])
        f1[:, cols(t)] = acc

    relay(5)
    for d in far:
        for p in range(4):
            pass_on[d][p, 2].wait_recv()
            pass_on[d][p, 3].wait_recv()

    @pl.loop(0, tiles)
    def _(t):
        acc = f1[:, cols(t)]
        for c in range(2 * per, chunks):
            acc += dot(hid[c], ffw[c * TILE : (c + 1) * TILE, cols(t)])
        f1[:, cols(t)] = acc

    c_cot.wait()
    cs[...] = jnp.zeros_like(cs)

    @pl.loop(0, rows // BLOCK)
    def _(i):
        r = cols(i, BLOCK)
        pos = lax.broadcasted_iota(jnp.int32, (BLOCK, width), 0) + i * BLOCK
        keep = (pos > 0) & (pos < length) & (pos != sep0) & (pos != sep1)
        x = f0[r, :] * small[5:6, :] + small[6:7, :] + f1[r, :] + small[7:8, :]
        x = x - mean_rows(x)
        scale = lax.rsqrt(mean_rows(x * x) + eps_norm)
        normed = x * scale
        act[r, :] = (normed * small[8:9, :] + small[9:10, :]).astype(BF16)
        g = jnp.where(keep, cotb[r, :].astype(F32), 0.0)
        s = g * small[8:9, :]
        gs = scale * (s - mean_rows(s) - normed * mean_rows(s * normed))
        low = gs.astype(BF16)
        f2[r, :] = gs
        a1[r, :] = low
        cs[0] += fold8(g)
        cs[1] += fold8(low.astype(F32))

    c_act = load(5, act, act_out)

    @pl.loop(0, chunks)
    def _(c):
        gi = (dot_nt(a1[...], ffw[cols(c), :]) * slope[c]).astype(BF16)
        hid[c] = gi
        s = total8(gi.astype(F32))
        ginb[2 * c] = s[:, :LANES]
        ginb[2 * c + 1] = s[:, LANES:]

    @pl.loop(0, tiles)
    def _(t):
        acc = dot_nt(hid[0], inw[0, cols(t), :])
        for c in range(1, chunks):
            acc += dot_nt(hid[c], inw[c, cols(t), :])
        f1[:, cols(t)] = acc

    @pl.loop(0, rows // BLOCK)
    def _(i):
        r = cols(i, BLOCK)
        g = f1[r, :] + f2[r, :]
        s = g * small[5:6, :]
        normed = f0[r, :]
        gs = sc1[r, 0:1] * (s - mean_rows(s) - normed * mean_rows(s * normed))
        low = gs.astype(BF16)
        f2[r, :] = gs
        a0[r, :] = low
        cs[2] += fold8(g)
        cs[3] += fold8(low.astype(F32))

    for i in range(4):
        tsum[0, i : i + 1, :] = total8(cs[i])
    peers = [(s, place(s // 2, s % 2)) for s in range(1, group)]
    t_sum = [remote(tsum.at[0], tsum.at[s], dev) for s, dev in peers]
    t_inb = [remote(ginb.at[pl.ds(s * brow, brow)], rinb.at[s], dev) for s, dev in peers]
    d_sum = [remote(sbuf.at[b], srec.at[b], rank(bit)) for b, bit in enumerate(bits)]
    d_inb = [remote(ibuf.at[b], irec.at[b], rank(bit)) for b, bit in enumerate(bits)]
    t_qv = [remote(tqv.at[0], tqv.at[s], dev) for s, dev in peers]
    d_qv = [remote(qbuf.at[b], qrec.at[b], rank(bit)) for b, bit in enumerate(bits)]
    steps = len(bits) + 1

    def over_tensor(ref):
        acc = None
        for t in range(group):
            s = (y - t // 2 + line) % line * 2 + (core + t) % 2
            acc = ref[s] if acc is None else acc + ref[s]
        return acc

    def reduce_sums(step):
        if step == 0:
            for c in t_sum + t_inb:
                c.wait_recv()
            sbuf[0] = over_tensor(tsum)
            for r in range(brow):
                u = natural(r // prow) * prow + r % prow
                acc = ginb[r] + rinb[1, r]
                for s in range(2, group):
                    acc += rinb[s, u]
                ibuf[0, r] = acc
        else:
            d_sum[step - 1].wait_recv()
            d_inb[step - 1].wait_recv()
            sbuf[step] = sbuf[step - 1] + srec[step - 1]
            ibuf[step] = ibuf[step - 1] + irec[step - 1]
        if step < steps - 1:
            d_sum[step].start()
            d_inb[step].start()

    def reduce_qv(step):
        if step == 0:
            for c in t_qv:
                c.wait_recv()
            qbuf[0] = over_tensor(tqv)
        else:
            d_qv[step - 1].wait_recv()
            qbuf[step] = qbuf[step - 1] + qrec[step - 1]
        if step < steps - 1:
            d_qv[step].start()

    for c in t_sum + t_inb:
        c.start()

    @pl.loop(0, tiles)
    def _(n):
        a1[:, cols(n)] = dot_nt(a0[...], outw[cols(n), :]).astype(BF16)

    @pl.loop(0, tiles)
    def _(n):
        kt = k[n].T
        dqs, dks, dvs = [], [], []
        for p in range(TILE // LANES):
            v2 = v[n, :, p * LANES : (p + 1) * LANES]
            qs = halves(q[n, :, p * LANES : (p + 1) * LANES])
            gs = halves(a1[:, cols(2 * n + p, LANES)])
            dk, dv = None, None
            for e in range(2):
                h = 2 * p + e
                dprob = dot_nt(v2, gs[e])
                low = pt[n * heads + h]
                prob = low.astype(F32)
                t = prob * dprob
                ds = (t - prob * jnp.sum(t, axis=0, keepdims=True)).astype(BF16)
                dvh = dot(low, gs[e])
                dkh = dot(ds, qs[e])
                dv = dvh if dv is None else dv + dvh
                dk = dkh if dk is None else dk + dkh
                dqs.append(dot(kt[h * hd : (h + 1) * hd], ds))
            dks.append(dk)
            dvs.append(dv)
        dq = (jnp.concatenate(dqs, axis=0) * hd**-0.5).astype(BF16).T
        dv = jnp.concatenate(dvs, axis=1).astype(BF16)
        q[n] = dq
        k[n] = jnp.concatenate(dks, axis=1).astype(BF16)
        v[n] = dv
        csqv[0, :, cols(n)] = fold8(dq.astype(F32))
        csqv[1, :, cols(n)] = fold8(dv.astype(F32))
        for s in range(min(steps, tiles)):

            @pl.when(n == s)
            def _(s=s):
                reduce_sums(s)

    for s in range(tiles, steps):
        reduce_sums(s)
    for i in range(2):
        tqv[0, i : i + 1, :] = total8(csqv[i])
    for c in t_qv:
        c.start()

    @pl.loop(0, tiles)
    def _(t):
        acc = f2[:, cols(t)]
        for n in range(tiles):
            for i, ref in enumerate((q, k, v)):
                acc += dot_nt(ref[n], qkvw[n + i * tiles, cols(t), :])
        f1[:, cols(t)] = acc
        for s in range(tiles - 1):

            @pl.when(t == s + 1)
            def _(s=s):
                reduce_qv(s)

    c_grad = load(6, f1, grad_out)
    for s in range(tiles - 1, steps):
        reduce_qv(s)
    shift2_out[...] = sbuf[steps - 1, 0:1]
    ffnb_out[...] = sbuf[steps - 1, 1:2]
    shift1_out[...] = sbuf[steps - 1, 2:3]
    outb_out[...] = sbuf[steps - 1, 3:4]
    inb_out[...] = ibuf[steps - 1]
    qv_out[...] = qbuf[steps - 1]

    for d in far:
        for c in direct[d] + to_x[d] + to_z[d] + list(pass_on[d].values()):
            c.wait_send()
    for c in core_in + [core_ffn] + bias + t_sum + t_inb + d_sum + d_inb + t_qv + d_qv:
        c.wait_send()
    c_act.wait()
    c_grad.wait()
    assert count[0] <= send.shape[0]


def step(
    ranks, group,
    tokens, segments, separators, lengths, type_table, qkv_weight, qv_bias, out_weight, out_bias, gain_one, shift_one,
    in_weight, in_bias, ffn_weight, ffn_bias, gain_two, shift_two, cotangent,
):
    pairs, rows, width = tokens.shape
    units = in_weight.shape[1]
    hidden = units * group
    chunks, tiles = hidden // TILE, width // TILE
    brow = units // LANES
    stages = ranks.bit_length() - 1
    line = group // 2
    copies = (line - 1) * 32 + units // TILE + 1 + 4 * (group - 1) + 3 * stages
    rowsets = (type_table, qv_bias, out_bias, gain_one, shift_one, ffn_bias, gain_two, shift_two)
    small = jnp.concatenate([x.astype(F32).reshape(-1, width) for x in rowsets], axis=0)
    V = pltpu.VMEM
    inside = pl.BlockSpec(memory_space=V)
    outside = pl.BlockSpec(memory_space=pl.ANY)
    scalar = pl.BlockSpec(memory_space=pltpu.SMEM)
    vector = jax.ShapeDtypeStruct((1, width), F32)
    act, grad, qv, outb, shift1, inb, ffnb, shift2 = pl.pallas_call(
        functools.partial(kernel, ranks, group),
        out_shape=(
            jax.ShapeDtypeStruct((rows, width), BF16),
            jax.ShapeDtypeStruct((rows, width), F32),
            jax.ShapeDtypeStruct((2, width), F32),
            vector,
            vector,
            jax.ShapeDtypeStruct((brow, 1, LANES), F32),
            vector,
            vector,
        ),
        in_specs=[scalar, scalar, inside] + [outside] * 7,
        out_specs=(outside, outside) + (inside,) * 6,
        scratch_shapes=[
            V((3 * tiles, width, TILE), BF16),
            V((width, width), BF16),
            V((chunks, width, TILE), BF16),
            V((hidden, width), BF16),
            V((hidden // LANES, 1, LANES), F32),
            V((tiles, rows, TILE), BF16),
            V((tiles, rows, TILE), BF16),
            V((tiles, rows, TILE), BF16),
            V((HEADS, rows, rows), BF16),
            V((chunks, rows, TILE), F32),
            V((chunks, rows, TILE), BF16),
            V((rows, width), BF16),
            V((rows, width), BF16),
            V((rows, width), F32),
            V((rows, width), F32),
            V((rows, width), F32),
            V((rows, width), BF16),
            V((rows, width), BF16),
            V((rows, width), BF16),
            V((rows, LANES), F32),
            V((4, 8, width), F32),
            V((2, 8, width), F32),
            V((hidden // LANES, 1, LANES), F32),
            V((group, brow, 1, LANES), F32),
            V((stages + 1, brow, 1, LANES), F32),
            V((stages, brow, 1, LANES), F32),
            V((group, 4, width), F32),
            V((stages + 1, 4, width), F32),
            V((stages, 4, width), F32),
            V((group, 2, width), F32),
            V((stages + 1, 2, width), F32),
            V((stages, 2, width), F32),
            pltpu.SemaphoreType.DMA((3 * tiles + units // TILE,)),
            pltpu.SemaphoreType.DMA((8,)),
            pltpu.SemaphoreType.DMA((copies,)),
            pltpu.SemaphoreType.DMA((copies,)),
        ],
        compiler_params=pltpu.CompilerParams(collective_id=0, has_side_effects=True, vmem_limit_bytes=67043328),
    )(
        lengths,
        separators,
        small,
        in_bias.astype(F32).reshape(brow, 1, LANES),
        tokens.reshape(rows, width),
        cotangent.reshape(rows, width),
        qkv_weight,
        out_weight,
        in_weight,
        ffn_weight,
    )
    return (
        act.reshape(pairs, rows, width),
        grad.reshape(pairs, rows, width),
        qv,
        outb.reshape(width),
        shift1.reshape(width),
        inb.reshape(units),
        ffnb.reshape(width),
        shift2.reshape(width),
    )


def solution(mesh):
    both = ("dp", "tensor")
    rows = P(both, None, None)
    return jax.shard_map(
        functools.partial(step, mesh.shape["dp"], mesh.shape["tensor"]),
        mesh=mesh,
        in_specs=(rows, P(both, None), P(both, None), P(both))
        + (P(),) * 7
        + (P(None, "tensor"), P("tensor"), P("tensor", None))
        + (P(),) * 3
        + (rows,),
        out_specs=(rows, rows, P(), P(), P(), P("tensor"), P(), P()),
        check_vma=False,
    )
```

time: 416 us -> 122 us (0.29); the launches traced: 408 us -> 122 us
  waiting for transfers between devices: 189 us -> 0 us
  Pallas kernels: 0 us -> 107 us
  matrix products: 80.6 us -> 0 us
  blocking collectives: 62 us -> 0 us
  other arithmetic: 37.9 us -> 4.01 us
  between operations: 15.2 us -> 1.33 us
  local copies, waits for them, and re-layouts: 23 us -> 10 us
    reduce_scatter x2 -> x0, waiting for transfers between devices: 117 us -> none  [the longest x1 69 us: local(): lax.psum_scatter(jnp.einsum('psf,fd->psd', rows, ffn_weight, preferred_el...]
    pallas_call x0 -> x1, Pallas kernels: none -> 107 us  [step(): pl.pallas_call(functools.partial(kernel, ranks, group), out_shape=(jax.Sh...]
    dot_general x14 -> x0, matrix products: 80.6 us -> none  [the longest x1 13 us: attend_backward(): jnp.einsum('qhd,khd->hqk', grad_mixed, value, preferred_element_type=jnp....]
    all_gather x2 -> x0, waiting for transfers between devices: 71.7 us -> none  [the longest x1 37.1 us: local(): lax.all_gather(first_low.reshape(pairs, seq, width), 'tensor', axis=0, ti...]
    psum x2 -> x0, blocking collectives: 62 us -> none  [the longest x1 39.9 us: local(): lax.psum((grad_qv, grad_out_bias, grad_shift_one, grad_ffn_bias, grad_shi...]
    convert_element_type x11 -> x0, other arithmetic: 22.6 us -> none  [the longest x1 12.6 us: attend_backward(): grad_scores = (probs * (grad_probs - inner_sum)).astype(jnp.bfloat16)]
    reduce_sum x9 -> x0, other arithmetic: 15.3 us -> none  [the longest x2 5.05 us: norm_backward(): centered = scaled - jnp.mean(scaled, axis=-1, keepdims=True)]
    unnamed x50 -> x22, local copies, waits for them, and re-layouts: 12.9 us -> 7.33 us
  transfers between devices with their start and end apart: 4 -> 0, of which waited for: 4 -> 0; matrix products, arithmetic and copies ran while one was open for 1% -> 0% of each run, Pallas kernels for 0% -> 0%
where the time goes in v2:
time: 122 us
  Pallas kernels  107 us (88%)
  local copies, waits for them, and re-layouts  10 us (8%)
  other arithmetic  4.01 us (3%)
  between operations  1.33 us (1%)
    pallas_call x1, Pallas kernels, step(): pl.pallas_call(functools.partial(kernel, ranks, group), out_shape=(jax.Sh...  107 us
    unnamed x22, local copies, waits for them, and re-layouts  7.33 us
    reshape x4, other arithmetic, step(): x.astype(F32).reshape(-1, width)  2.73 us
    concatenate x1, local copies, waits for them, and re-layouts, step(): jnp.concatenate([x.astype(F32).reshape(-1, width) for x in rowsets], axis=0)  2.68 us

profile of v2, /device:TPU:0, one launch (start us, length us, event | category | flops | bytes accessed | tf_op | source)
XLA Modules:
  0.0 121.9 jit_solution(7004673944509849757)
XLA Ops:
  1.3 0.7 reshape.99
  2.0 0.7 reshape.101
  2.6 1.3 %reshape.107 = f32[1024]{0:T(1024)} convert(bf16[1024]{0:T(1024)(128)(2,1)} %param.29) | non-fusion elementwise | flops 1024 | bytes 6144 | tf_op jit(solution)/shard_map/reshape | solution.py:570
  3.9 0.7 reshape.103
  4.6 0.7 reshape.105
  5.3 2.7 %concatenate.3.small = f32[10,1024]{1,0:T(8,128)} concatenate(bf16[2,1024]{1,0:T(2,128)(2,1)} %param.21, bf16[2,1024]{1,0:T(2,128)(2,1)} %param.23, f32[1,1024]{1,0:T(1,128)S(1)} %bitcast.21, f32[1,1024]{1,0:T(1,128)} %bitcast.25, f32[1,1024]{1,0:T(1,128)S(1)} %bitcast.22, f32[1,1024]{1,0:T(1,128)S(1)} %bitcast.23, f32[1,1024]{1,0:T(1,128)} %bitcast.26, f32[1,1024]{1,0:T(1,128)S(1)} %bitcast.24), dimensions={0} | concatenate | bytes 73728 | tf_op jit(solution)/shard_map/concatenate | solution.py:507
  8.0 106.5 %shard_map.224 = (bf16[512,1024]{1,0:T(8,128)(2,1)}, f32[512,1024]{1,0:T(8,128)}, f32[2,1024]{1,0:T(2,128)}, f32[1,1024]{1,0:T(1,128)}, f32[1,1024]{1,0:T(1,128)...) custom-call(s32[1]{0:T(128)S(6)} %copy.33.lengths, s32[1,2]{1,0:T(1,128)} %separators.1, ...), custom_call_target="tpu_custom_call" | custom-call | tf_op jit(solution)/shard_map/pallas_call | solution.py:513
  114.5 0.0 copy-start
  114.5 2.4 %copy.34 = bf16[1,512,1024]{2,1,0:T(8,128)(2,1)} copy(bf16[1,512,1024]{2,1,0:T(8,128)(2,1)} %bitcast.17) | data formatting | bytes 2097152
  117.0 0.0 copy-done
  117.0 0.0 copy-start.1
  117.0 0.0 copy-start.6
  117.0 0.0 copy-start.5
  117.0 0.0 copy-start.4
  117.0 0.0 copy-start.3
  117.0 0.0 copy-start.2
  117.0 1.3 %copy.35 = f32[1,512,1024]{2,1,0:T(8,128)} copy(f32[1,512,1024]{2,1,0:T(8,128)S(1)} %bitcast.16) | data formatting | bytes 4194304
  118.3 0.0 copy-done.1
  118.3 0.6 copy.36
  118.9 0.0 copy-done.6
  118.9 0.6 copy.37
  119.5 0.0 copy-done.5
  119.5 0.6 copy.38
  120.1 0.0 copy-done.4
  120.1 0.6 copy.39
  120.7 0.0 copy-done.3
  120.7 0.6 copy.40
  121.3 0.0 copy-done.2
  121.3 0.6 copy.41
Async XLA Ops:
  114.5 2.4 %copy-start = (f32[512,1024]{1,0:T(8,128)S(1)}, f32[512,1024]{1,0:T(8,128)}, u32[]{:S(2)}) copy-start(f32[512,1024]{1,0:T(8,128)} %get-tuple-element.17) | copy-start | bytes 6291460
  117.0 1.4 %copy-start.1 = (f32[2,1024]{1,0:T(2,128)S(1)}, f32[2,1024]{1,0:T(2,128)}, u32[]{:S(2)}) copy-start(f32[2,1024]{1,0:T(2,128)} %get-tuple-element.34) | copy-start | bytes 24580
  117.0 2.0 %copy-start.6 = (f32[1,1024]{1,0:T(1,128)S(1)}, f32[1,1024]{1,0:T(1,128)}, u32[]{:S(2)}) copy-start(f32[1,1024]{1,0:T(1,128)} %get-tuple-element.19) | copy-start | bytes 12292
  117.0 2.6 %copy-start.5 = (f32[1,1024]{1,0:T(1,128)S(1)}, f32[1,1024]{1,0:T(1,128)}, u32[]{:S(2)}) copy-start(f32[1,1024]{1,0:T(1,128)} %get-tuple-element.20) | copy-start | bytes 12292
  117.0 3.1 %copy-start.4 = (f32[8,1,128]{2,1,0:T(1,128)S(1)}, f32[8,1,128]{2,1,0:T(1,128)}, u32[]{:S(2)}) copy-start(f32[8,1,128]{2,1,0:T(1,128)} %get-tuple-element.21) | copy-start | bytes 12292
  117.0 3.7 %copy-start.3 = (f32[1,1024]{1,0:T(1,128)S(1)}, f32[1,1024]{1,0:T(1,128)}, u32[]{:S(2)}) copy-start(f32[1,1024]{1,0:T(1,128)} %get-tuple-element.22) | copy-start | bytes 12292
  117.0 4.3 %copy-start.2 = (f32[1,1024]{1,0:T(1,128)S(1)}, f32[1,1024]{1,0:T(1,128)}, u32[]{:S(2)}) copy-start(f32[1,1024]{1,0:T(1,128)} %get-tuple-element.23) | copy-start | bytes 12292

commit v3 on v2

--- a/solution.py
+++ b/solution.py
@@ -51,11 +51,11 @@
 
 def kernel(
     ranks, group,
-    lengths, separators, small, in_b, tokens, cot, qkv_w, out_w, in_w, ffn_w,
-    act_out, grad_out, qv_out, outb_out, shift1_out, inb_out, ffnb_out, shift2_out,
+    lengths, separators, table, qv_b, out_b, gain1, shift1, ffn_b, gain2, shift2, in_b, tokens, cot, qkv_w, out_w, in_w, ffn_w,
+    act_out, grad_out, sums_out, qv_out, inb_out,
     qkvw, outw, inw, ffw, inb, q, k, v, pt, slope, hid, a0, a1, f0, f1, f2, tok, cotb, act, sc1, cs, csqv,
-    ginb, rinb, ibuf, irec, tsum, sbuf, srec, tqv, qbuf, qrec,
-    wsem, lsem, send, recv,
+    small, ginb, rinb, ibuf, tsum, sbuf, tqv, qbuf,
+    raw, inraw, wsem, lsem, send, recv,
 ):
     rows, width = tok.shape
     tiles = width // TILE
@@ -71,16 +71,21 @@
     sep0, sep1 = separators[0, 0], separators[0, 1]
     dp, tensor = lax.axis_index("dp"), lax.axis_index("tensor")
     y, core = tensor // 2, tensor % 2
-    bits = [1 << b for b in range(ranks.bit_length() - 1)]
+    near = min(ranks, 8)
+    bits = [1 << b for b in range(near.bit_length() - 1)]
+    wide = [1 << b for b in range(ranks.bit_length() - 1) if 1 << b >= near]
 
     def place(d, other):
         return (dp, (y + d + line) % line * 2 + (core + other) % 2)
 
-    def rank(bit):
-        return (flip(dp, bit), tensor)
+    def mixed(offset):
+        return sum((offset // b + dp // b) % 2 * b for b in bits)
+
+    def rank(offset):
+        return (dp // near * near + mixed(offset) if offset < near else flip(dp, offset), tensor)
 
     barrier = pltpu.get_barrier_semaphore()
-    friends = [place(s // 2, s % 2) for s in range(1, group)] + [rank(b) for b in bits]
+    friends = [place(s // 2, s % 2) for s in range(1, group)] + [rank(o) for o in list(range(1, near)) + wide]
     for f in friends:
         pl.semaphore_signal(barrier, inc=1, device_id=f, device_id_type=MESH)
 
@@ -113,6 +118,7 @@
         c.start()
         return c
 
+    c_small = [load(8 + i, src, dst) for i, (src, dst) in enumerate(zip((table, qv_b, out_b, gain1, shift1, ffn_b, gain2, shift2), raw))]
     c_tok = load(0, tokens, tok)
     c_qkv = []
     for n in range(3 * tiles):
@@ -126,7 +132,7 @@
         c_in.append(c)
     c_out = load(1, out_w, outw)
     c_ffn = load(2, ffn_w, ffw.at[pl.ds(0, units), :])
-    c_b = load(3, in_b, inb.at[pl.ds(0, brow)])
+    c_b = load(3, in_b, inraw[0])
     c_cot = load(4, cot, cotb)
 
     far = range(1, line)
@@ -136,41 +142,58 @@
     pass_on = {d: {(p, i): remote(piece(2 * d, p, i), piece(2 * d + 1, p, i), place(0, 1)) for p in range(4) for i in range(4)} for d in far}
     core_in = [remote(in_w.at[:, n * TILE : (n + 1) * TILE], inw.at[per + n], place(0, 1)) for n in range(per)]
     core_ffn = remote(ffn_w, ffw.at[pl.ds(units, units), :], place(0, 1))
-    bias = [remote(in_b, inb.at[pl.ds(s * brow, brow)], place(-(s // 2), s % 2)) for s in range(1, group)]
+    bias = [remote(in_b, inraw[s], place(-(s // 2), s % 2)) for s in range(1, group)]
 
     def relay(step):
         for d in far:
             yd, xd, zd, on = direct[d], to_x[d], to_z[d], pass_on[d]
-            if step < 4:
-                yd[step].wait_recv()
-                xd[step].start()
-                zd[step].start()
-                on[0, step].start()
-            if step == 1:
+            if step in ("0", "1", "2", "3"):
+                i = int(step)
+                yd[i].wait_recv()
+                xd[i].start()
+                zd[i].start()
+                on[0, i].start()
+            if step == "in0":
                 zd[0].wait_recv()
                 xd[4].start()
                 on[2, 0].start()
                 xd[0].wait_recv()
                 on[1, 0].start()
-            if step == 2:
+            if step == "in1":
                 xd[1].wait_recv()
                 zd[4].start()
                 on[1, 1].start()
                 zd[1].wait_recv()
                 on[2, 1].start()
-            if step == 3:
+            if step == "in":
                 xd[4].wait_recv()
                 on[3, 0].start()
                 zd[4].wait_recv()
                 on[3, 1].start()
-            if step >= 4:
-                yd[step].wait_recv()
-                on[3, step - 2].start()
-                xd[step - 2].wait_recv()
-                on[1, step - 2].start()
-                zd[step - 2].wait_recv()
-                on[2, step - 2].start()
-
+            if step in ("4", "5"):
+                i = int(step)
+                yd[i].wait_recv()
+                on[3, i - 2].start()
+                xd[i - 2].wait_recv()
+                on[1, i - 2].start()
+                zd[i - 2].wait_recv()
+                on[2, i - 2].start()
+
+    pl.semaphore_wait(barrier, len(friends))
+    for c in bias:
+        c.start()
+    for d in far:
+        for c in direct[d]:
+            c.start()
+    for c in core_in + [core_ffn]:
+        c.start()
+
+    for c in c_small:
+        c.wait()
+    small[0:2, :] = raw[0][...].astype(F32)
+    small[2:4, :] = raw[1][...].astype(F32)
+    for i in range(2, 8):
+        small[2 + i : 3 + i, :] = raw[i][...].astype(F32).reshape(1, width)
     c_tok.wait()
 
     @pl.loop(0, rows // BLOCK)
@@ -182,29 +205,28 @@
         f0[r, :] = e
         a0[r, :] = e.astype(BF16)
 
-    pl.semaphore_wait(barrier, len(friends))
-    for d in far:
-        for c in direct[d]:
-            c.start()
-    for c in core_in + [core_ffn] + bias:
-        c.start()
-
-    for c in c_qkv:
+    for c in c_qkv[:tiles]:
         c.wait()
 
     @pl.loop(0, tiles)
     def _(n):
         q[n] = (dot(a0[...], qkvw[n]) + small[2:3, cols(n)]).astype(BF16) * jnp.asarray(hd**-0.5, BF16)
 
+    for c in c_qkv[tiles : 2 * tiles]:
+        c.wait()
+
     @pl.loop(0, tiles)
     def _(n):
         k[n] = dot(a0[...], qkvw[n + tiles]).astype(BF16)
 
+    for c in c_qkv[2 * tiles :]:
+        c.wait()
+
     @pl.loop(0, tiles)
     def _(n):
         v[n] = (dot(a0[...], qkvw[n + 2 * tiles]) + small[3:4, cols(n)]).astype(BF16)
 
-    relay(0)
+    relay("0")
 
     low_half = lax.broadcasted_iota(jnp.int32, (rows, LANES), 1) < hd
     zero = jnp.zeros((rows, LANES), BF16)
@@ -231,15 +253,22 @@
                 outs.append(dot(vt[h * hd : (h + 1) * hd], prob))
         a1[:, cols(n)] = jnp.concatenate(outs, axis=0).astype(BF16).T
 
-        @pl.when(n == tiles // 2)
+        @pl.when(n == 1)
         def _():
-            relay(1)
+            relay("1")
+
+        @pl.when(n == 2)
+        def _():
+            relay("in0")
 
     c_out.wait()
 
     @pl.loop(0, tiles)
     def _(n):
         f1[:, cols(n)] = dot(a1[...], outw[:, cols(n)]) + small[4:5, cols(n)] + f0[:, cols(n)]
+
+    relay("in1")
+    relay("2")
 
     @pl.loop(0, rows // BLOCK)
     def _(i):
@@ -252,8 +281,6 @@
         a0[r, :] = (normed * small[5:6, :] + small[6:7, :]).astype(BF16)
         sc1[r, :] = jnp.broadcast_to(scale, (BLOCK, LANES))
 
-    relay(2)
-
     def hidden_units(c, first, second):
         x = dot(a0[...], inw[c]) + jnp.concatenate([inb[first], inb[second]], axis=1)
         cdf = 0.5 * (1.0 + lax.erf(x * root_half))
@@ -264,25 +291,38 @@
         c.wait()
     for c in core_in + bias:
         c.wait_recv()
+    for t in range(group):
+        b = inraw[t][...].astype(F32).reshape(1, units)
+        for r in range(brow):
+            inb[t * brow + r] = b[:, r * LANES : (r + 1) * LANES]
 
     @pl.loop(0, 2 * per)
     def _(c):
         hidden_units(c, 2 * c, 2 * c + 1)
 
-    relay(3)
-    for d in far:
-        for p in range(4):
-            pass_on[d][p, 0].wait_recv()
-            pass_on[d][p, 1].wait_recv()
+        @pl.when(c == 2 * per - 4)
+        def _():
+            relay("3")
 
     def shuffled(r):
         return r // brow * brow + natural(r % brow // prow) * prow + r % prow
 
-    @pl.loop(2 * per, chunks)
-    def _(c):
-        hidden_units(c, shuffled(2 * c), shuffled(2 * c + 1))
-
-    relay(4)
+    def units_of(i):
+        for d in far:
+            for p in range(4):
+                if (p * part) // TILE == i:
+                    pass_on[d][p, 0].wait_recv()
+                    pass_on[d][p, 1].wait_recv()
+
+        @pl.loop(2, group)
+        def _(t):
+            c = t * per + i
+            hidden_units(c, shuffled(2 * c), shuffled(2 * c + 1))
+
+    early = per - 1
+    for i in range(early):
+        units_of(i)
+    relay("in")
     c_ffn.wait()
     core_ffn.wait_recv()
 
@@ -293,7 +333,10 @@
             acc += dot(hid[c], ffw[c * TILE : (c + 1) * TILE, cols(t)])
         f1[:, cols(t)] = acc
 
-    relay(5)
+    relay("4")
+    for i in range(early, per):
+        units_of(i)
+    relay("5")
     for d in far:
         for p in range(4):
             pass_on[d][p, 2].wait_recv()
@@ -363,11 +406,18 @@
     peers = [(s, place(s // 2, s % 2)) for s in range(1, group)]
     t_sum = [remote(tsum.at[0], tsum.at[s], dev) for s, dev in peers]
     t_inb = [remote(ginb.at[pl.ds(s * brow, brow)], rinb.at[s], dev) for s, dev in peers]
-    d_sum = [remote(sbuf.at[b], srec.at[b], rank(bit)) for b, bit in enumerate(bits)]
-    d_inb = [remote(ibuf.at[b], irec.at[b], rank(bit)) for b, bit in enumerate(bits)]
+    hops = [list(range(1, near))] + [[w] for w in wide]
+    steps = len(hops) + 1
+
+    def spread(ref):
+        copies, base = [], 0
+        for hop in hops:
+            copies.append([remote(ref.at[base], ref.at[base + i + 1], rank(o)) for i, o in enumerate(hop)])
+            base += len(hop) + 1
+        return copies
+
+    d_sum, d_inb, d_qv = spread(sbuf), spread(ibuf), spread(qbuf)
     t_qv = [remote(tqv.at[0], tqv.at[s], dev) for s, dev in peers]
-    d_qv = [remote(qbuf.at[b], qrec.at[b], rank(bit)) for b, bit in enumerate(bits)]
-    steps = len(bits) + 1
 
     def over_tensor(ref):
         acc = None
@@ -376,36 +426,51 @@
             acc = ref[s] if acc is None else acc + ref[s]
         return acc
 
+    def over_hop(ref, hop):
+        if hop == 0:
+            acc = ref[mixed(0)]
+            for o in range(1, near):
+                acc += ref[mixed(o)]
+            return acc
+        base = near + 2 * (hop - 1)
+        return ref[base] + ref[base + 1]
+
+    def go(step, buffers, copies, totals):
+        if step == 0:
+            for ref, value in zip(buffers, totals()):
+                ref[0] = value
+        else:
+            for ref, cs_ in zip(buffers, copies):
+                for c in cs_[step - 1]:
+                    c.wait_recv()
+                ref[near + 2 * (step - 1)] = over_hop(ref, step - 1)
+        if step < steps - 1:
+            for cs_ in copies:
+                for c in cs_[step]:
+                    c.start()
+
+    def first_sums():
+        for c in t_sum + t_inb:
+            c.wait_recv()
+        parts = []
+        for r in range(brow):
+            u = natural(r // prow) * prow + r % prow
+            acc = ginb[r] + rinb[1, r]
+            for s in range(2, group):
+                acc += rinb[s, u]
+            parts.append(acc)
+        return over_tensor(tsum), jnp.stack(parts)
+
+    def first_qv():
+        for c in t_qv:
+            c.wait_recv()
+        return (over_tensor(tqv),)
+
     def reduce_sums(step):
-        if step == 0:
-            for c in t_sum + t_inb:
-                c.wait_recv()
-            sbuf[0] = over_tensor(tsum)
-            for r in range(brow):
-                u = natural(r // prow) * prow + r % prow
-                acc = ginb[r] + rinb[1, r]
-                for s in range(2, group):
-                    acc += rinb[s, u]
-                ibuf[0, r] = acc
-        else:
-            d_sum[step - 1].wait_recv()
-            d_inb[step - 1].wait_recv()
-            sbuf[step] = sbuf[step - 1] + srec[step - 1]
-            ibuf[step] = ibuf[step - 1] + irec[step - 1]
-        if step < steps - 1:
-            d_sum[step].start()
-            d_inb[step].start()
+        go(step, (sbuf, ibuf), (d_sum, d_inb), first_sums)
 
     def reduce_qv(step):
-        if step == 0:
-            for c in t_qv:
-                c.wait_recv()
-            qbuf[0] = over_tensor(tqv)
-        else:
-            d_qv[step - 1].wait_recv()
-            qbuf[step] = qbuf[step - 1] + qrec[step - 1]
-        if step < steps - 1:
-            d_qv[step].start()
+        go(step, (qbuf,), (d_qv,), first_qv)
 
     for c in t_sum + t_inb:
         c.start()
@@ -464,30 +529,51 @@
             for i, ref in enumerate((q, k, v)):
                 acc += dot_nt(ref[n], qkvw[n + i * tiles, cols(t), :])
         f1[:, cols(t)] = acc
-        for s in range(tiles - 1):
+        for s in range(min(steps, tiles - 1)):
 
             @pl.when(t == s + 1)
             def _(s=s):
                 reduce_qv(s)
 
     c_grad = load(6, f1, grad_out)
-    for s in range(tiles - 1, steps):
+    for s in range(min(steps, tiles - 1), steps):
         reduce_qv(s)
-    shift2_out[...] = sbuf[steps - 1, 0:1]
-    ffnb_out[...] = sbuf[steps - 1, 1:2]
-    shift1_out[...] = sbuf[steps - 1, 2:3]
-    outb_out[...] = sbuf[steps - 1, 3:4]
-    inb_out[...] = ibuf[steps - 1]
-    qv_out[...] = qbuf[steps - 1]
+    last = near + 2 * (steps - 2)
+    outs = [load(7, sbuf.at[last], sums_out), load(16, qbuf.at[last], qv_out), load(17, ibuf.at[last], inb_out)]
 
     for d in far:
         for c in direct[d] + to_x[d] + to_z[d] + list(pass_on[d].values()):
             c.wait_send()
-    for c in core_in + [core_ffn] + bias + t_sum + t_inb + d_sum + d_inb + t_qv + d_qv:
+    for c in core_in + [core_ffn] + bias + t_sum + t_inb + t_qv + sum(d_sum + d_inb + d_qv, []):
         c.wait_send()
-    c_act.wait()
-    c_grad.wait()
+    for c in [c_act, c_grad] + outs:
+        c.wait()
     assert count[0] <= send.shape[0]
+
+
+def finish(act, grad, sums, qv, inb, act_out, grad_out, qv_out, outb_out, shift1_out, inb_out, ffnb_out, shift2_out, abuf, gbuf, sbuf, qbuf, ibuf, into, out):
+    pieces = 4
+    size = act.shape[0] // pieces
+    plan = [(sums, sbuf, None), (qv, qbuf, qv_out), (inb, ibuf, inb_out)]
+    for i in range(pieces):
+        r = pl.ds(i * size, size)
+        plan.append((grad.at[r, :], gbuf.at[r, :], grad_out.at[r, :]))
+        plan.append((act.at[r, :], abuf.at[r, :], act_out.at[r, :]))
+    first = [pltpu.make_async_copy(src, mid, into.at[i]) for i, (src, mid, _) in enumerate(plan)]
+    for c in first:
+        c.start()
+    second = []
+    for i, (_, mid, dst) in enumerate(plan):
+        first[i].wait()
+        if dst is not None:
+            second.append(pltpu.make_async_copy(mid, dst, out.at[i]))
+            second[-1].start()
+        else:
+            for j, ref in enumerate((shift2_out, ffnb_out, shift1_out, outb_out)):
+                second.append(pltpu.make_async_copy(mid.at[j : j + 1, :], ref, out.at[len(plan) + j]))
+                second[-1].start()
+    for c in second:
+        c.wait()
 
 
 def step(
@@ -500,30 +586,26 @@
     hidden = units * group
     chunks, tiles = hidden // TILE, width // TILE
     brow = units // LANES
-    stages = ranks.bit_length() - 1
     line = group // 2
-    copies = (line - 1) * 32 + units // TILE + 1 + 4 * (group - 1) + 3 * stages
-    rowsets = (type_table, qv_bias, out_bias, gain_one, shift_one, ffn_bias, gain_two, shift_two)
-    small = jnp.concatenate([x.astype(F32).reshape(-1, width) for x in rowsets], axis=0)
+    near = min(ranks, 8)
+    far_bits = (ranks // near).bit_length() - 1
+    slots = near + 2 * far_bits + 1
+    copies = (line - 1) * 32 + units // TILE + 1 + 4 * (group - 1) + 3 * (near - 1 + far_bits)
+    vectors = (type_table, qv_bias, out_bias, gain_one, shift_one, ffn_bias, gain_two, shift_two)
     V = pltpu.VMEM
-    inside = pl.BlockSpec(memory_space=V)
     outside = pl.BlockSpec(memory_space=pl.ANY)
     scalar = pl.BlockSpec(memory_space=pltpu.SMEM)
-    vector = jax.ShapeDtypeStruct((1, width), F32)
-    act, grad, qv, outb, shift1, inb, ffnb, shift2 = pl.pallas_call(
+    act, grad, sums, qv, inb = pl.pallas_call(
         functools.partial(kernel, ranks, group),
         out_shape=(
             jax.ShapeDtypeStruct((rows, width), BF16),
             jax.ShapeDtypeStruct((rows, width), F32),
+            jax.ShapeDtypeStruct((4, width), F32),
             jax.ShapeDtypeStruct((2, width), F32),
-            vector,
-            vector,
             jax.ShapeDtypeStruct((brow, 1, LANES), F32),
-            vector,
-            vector,
         ),
-        in_specs=[scalar, scalar, inside] + [outside] * 7,
-        out_specs=(outside, outside) + (inside,) * 6,
+        in_specs=[scalar, scalar] + [outside] * 15,
+        out_specs=(outside,) * 5,
         scratch_shapes=[
             V((3 * tiles, width, TILE), BF16),
             V((width, width), BF16),
@@ -547,18 +629,18 @@
             V((rows, LANES), F32),
             V((4, 8, width), F32),
             V((2, 8, width), F32),
+            V((10, width), F32),
             V((hidden // LANES, 1, LANES), F32),
             V((group, brow, 1, LANES), F32),
-            V((stages + 1, brow, 1, LANES), F32),
-            V((stages, brow, 1, LANES), F32),
+            V((slots, brow, 1, LANES), F32),
             V((group, 4, width), F32),
-            V((stages + 1, 4, width), F32),
-            V((stages, 4, width), F32),
+            V((slots, 4, width), F32),
             V((group, 2, width), F32),
-            V((stages + 1, 2, width), F32),
-            V((stages, 2, width), F32),
+            V((slots, 2, width), F32),
+            [V(x.shape, x.dtype) for x in vectors],
+            [V((units,), BF16)] * group,
             pltpu.SemaphoreType.DMA((3 * tiles + units // TILE,)),
-            pltpu.SemaphoreType.DMA((8,)),
+            pltpu.SemaphoreType.DMA((18,)),
             pltpu.SemaphoreType.DMA((copies,)),
             pltpu.SemaphoreType.DMA((copies,)),
         ],
@@ -566,8 +648,8 @@
     )(
         lengths,
         separators,
-        small,
-        in_bias.astype(F32).reshape(brow, 1, LANES),
+        *vectors,
+        in_bias,
         tokens.reshape(rows, width),
         cotangent.reshape(rows, width),
         qkv_weight,
@@ -575,6 +657,31 @@
         in_weight,
         ffn_weight,
     )
+    vector = jax.ShapeDtypeStruct((1, width), F32)
+    act, grad, qv, outb, shift1, inb, ffnb, shift2 = pl.pallas_call(
+        finish,
+        out_shape=(
+            jax.ShapeDtypeStruct((rows, width), BF16),
+            jax.ShapeDtypeStruct((rows, width), F32),
+            jax.ShapeDtypeStruct((2, width), F32),
+            vector,
+            vector,
+            jax.ShapeDtypeStruct((brow, 1, LANES), F32),
+            vector,
+            vector,
+        ),
+        in_specs=[outside] * 5,
+        out_specs=(outside,) * 8,
+        scratch_shapes=[
+            V((rows, width), BF16),
+            V((rows, width), F32),
+            V((4, width), F32),
+            V((2, width), F32),
+            V((brow, 1, LANES), F32),
+            pltpu.SemaphoreType.DMA((16,)),
+            pltpu.SemaphoreType.DMA((16,)),
+        ],
+    )(act, grad, sums, qv, inb)
     return (
         act.reshape(pairs, rows, width),
         grad.reshape(pairs, rows, width),

time: 122 us -> 97.6 us (0.80)
  Pallas kernels: 107 us -> 96 us
  local copies, waits for them, and re-layouts: 10 us -> 0 us
  other arithmetic: 4.01 us -> 0 us
    pallas_call x1, Pallas kernels: 107 us -> 93 us  [step(): pl.pallas_call(functools.partial(kernel, ranks, group), out_shape=(jax.Sh...]
    unnamed x22 -> x0, local copies, waits for them, and re-layouts: 7.33 us -> none
    reshape x5 -> x0, other arithmetic: 4.01 us -> none  [the longest x4 2.73 us: step(): x.astype(F32).reshape(-1, width)]
    pallas_call x0 -> x1, Pallas kernels: none -> 3.01 us  [step(): pl.pallas_call(finish, out_shape=(jax.ShapeDtypeStruct((rows, width), BF1...]
    concatenate x1 -> x0, local copies, waits for them, and re-layouts: 2.68 us -> none  [step(): jnp.concatenate([x.astype(F32).reshape(-1, width) for x in rowsets], axis=0)]
where the time goes in v3:
time: 97.6 us; the launch traced here: 97.3 us
  Pallas kernels  96 us (98%)
  between operations  1.29 us (1%)
    pallas_call x1, Pallas kernels, step(): pl.pallas_call(functools.partial(kernel, ranks, group), out_shape=(jax.Sh...  93 us
    pallas_call x1, Pallas kernels, step(): pl.pallas_call(finish, out_shape=(jax.ShapeDtypeStruct((rows, width), BF1...  3.01 us

profile of v3, /device:TPU:0, one launch (start us, length us, event | category | flops | bytes accessed | tf_op | source)
XLA Modules:
  0.0 97.3 jit_solution(1607755273581384417)
XLA Ops:
  1.3 93.0 %shard_map.224 = (bf16[512,1024]{1,0:T(8,128)(2,1)}, f32[512,1024]{1,0:T(8,128)}, f32[4,1024]{1,0:T(4,128)}, f32[2,1024]{1,0:T(2,128)}, f32[8,1,128]{2,1,0:T(1,128)}) custom-call(s32[1]{0:T(128)S(6)} %copy.25.lengths, s32[1,2]{1,0:T(1,128)} %separators.1, bf16[2,1024]{1,0:T(2,128)(2,1)} %table.1, bf16[2,1024]{1,0:T(2,128)(2,1)} %qv_b.1, ...), custom_call_target="tpu_custom_call" | custom-call | tf_op jit(solution)/shard_map/pallas_call | solution.py:598
  94.3 3.0 %shard_map.225 = (bf16[512,1024]{1,0:T(8,128)(2,1)}, f32[512,1024]{1,0:T(8,128)}, f32[2,1024]{1,0:T(2,128)}, f32[1,1024]{1,0:T(1,128)}, f32[1,1024]{1,0:T(1,128)...) custom-call(bf16[512,1024]{1,0:T(8,128)(2,1)} %get-tuple-element.21.act, ...), custom_call_target="tpu_custom_call" | custom-call | tf_op jit(solution)/shard_map/pallas_call | solution.py:661

commit v4 on v3

--- a/solution.py
+++ b/solution.py
@@ -55,7 +55,7 @@
     act_out, grad_out, sums_out, qv_out, inb_out,
     qkvw, outw, inw, ffw, inb, q, k, v, pt, slope, hid, a0, a1, f0, f1, f2, tok, cotb, act, sc1, cs, csqv,
     small, ginb, rinb, ibuf, tsum, sbuf, tqv, qbuf,
-    raw, inraw, wsem, lsem, send, recv,
+    raw, inraw, len_s, sep_s, wsem, lsem, send, recv,
 ):
     rows, width = tok.shape
     tiles = width // TILE
@@ -67,8 +67,6 @@
     brow = units // LANES
     prow = part // LANES
     per = units // TILE
-    length = lengths[0]
-    sep0, sep1 = separators[0, 0], separators[0, 1]
     dp, tensor = lax.axis_index("dp"), lax.axis_index("tensor")
     y, core = tensor // 2, tensor % 2
     near = min(ranks, 8)
@@ -120,6 +118,7 @@
 
     c_small = [load(8 + i, src, dst) for i, (src, dst) in enumerate(zip((table, qv_b, out_b, gain1, shift1, ffn_b, gain2, shift2), raw))]
     c_tok = load(0, tokens, tok)
+    c_small += [load(18, lengths, len_s), load(19, separators, sep_s)]
     c_qkv = []
     for n in range(3 * tiles):
         c = pltpu.make_async_copy(qkv_w.at[:, n * TILE : (n + 1) * TILE], qkvw.at[n], wsem.at[n])
@@ -190,13 +189,15 @@
 
     for c in c_small:
         c.wait()
+    length = len_s[0]
+    sep0, sep1 = sep_s[0, 0], sep_s[0, 1]
     small[0:2, :] = raw[0][...].astype(F32)
     small[2:4, :] = raw[1][...].astype(F32)
     for i in range(2, 8):
         small[2 + i : 3 + i, :] = raw[i][...].astype(F32).reshape(1, width)
     c_tok.wait()
 
-    @pl.loop(0, rows // BLOCK)
+    @pl.loop(0, rows // BLOCK, unroll=2)
     def _(i):
         r = cols(i, BLOCK)
         pos = lax.broadcasted_iota(jnp.int32, (BLOCK, width), 0) + i * BLOCK
@@ -208,21 +209,21 @@
     for c in c_qkv[:tiles]:
         c.wait()
 
-    @pl.loop(0, tiles)
+    @pl.loop(0, tiles, unroll=2)
     def _(n):
         q[n] = (dot(a0[...], qkvw[n]) + small[2:3, cols(n)]).astype(BF16) * jnp.asarray(hd**-0.5, BF16)
 
     for c in c_qkv[tiles : 2 * tiles]:
         c.wait()
 
-    @pl.loop(0, tiles)
+    @pl.loop(0, tiles, unroll=2)
     def _(n):
         k[n] = dot(a0[...], qkvw[n + tiles]).astype(BF16)
 
     for c in c_qkv[2 * tiles :]:
         c.wait()
 
-    @pl.loop(0, tiles)
+    @pl.loop(0, tiles, unroll=2)
     def _(n):
         v[n] = (dot(a0[...], qkvw[n + 2 * tiles]) + small[3:4, cols(n)]).astype(BF16)
 
@@ -261,16 +262,16 @@
         def _():
             relay("in0")
 
+    relay("2")
+
     c_out.wait()
 
-    @pl.loop(0, tiles)
+    @pl.loop(0, tiles, unroll=2)
     def _(n):
         f1[:, cols(n)] = dot(a1[...], outw[:, cols(n)]) + small[4:5, cols(n)] + f0[:, cols(n)]
 
-    relay("in1")
-    relay("2")
-
-    @pl.loop(0, rows // BLOCK)
+
+    @pl.loop(0, rows // BLOCK, unroll=2)
     def _(i):
         r = cols(i, BLOCK)
         x = f1[r, :]
@@ -281,6 +282,8 @@
         a0[r, :] = (normed * small[5:6, :] + small[6:7, :]).astype(BF16)
         sc1[r, :] = jnp.broadcast_to(scale, (BLOCK, LANES))
 
+    relay("in1")
+
     def hidden_units(c, first, second):
         x = dot(a0[...], inw[c]) + jnp.concatenate([inb[first], inb[second]], axis=1)
         cdf = 0.5 * (1.0 + lax.erf(x * root_half))
@@ -336,33 +339,61 @@
     relay("4")
     for i in range(early, per):
         units_of(i)
+    half = part // 2
+    blocks = [(t * units + p * part + h * half, h > 0 and p > 0) for t in range(2, group) for p in range(4) for h in range(2)]
+    if half % LANES:
+        ready, late = [], [u for u, _ in blocks]
+    else:
+        ready, late = [u for u, last in blocks if not last], [u for u, last in blocks if last]
+
+    def contract(t, acc, starts):
+        step = max(1, TILE // half)
+        for i in range(0, len(starts), step):
+            us = starts[i : i + step]
+            if us == list(range(us[0], us[0] + TILE, half)) and us[0] % TILE == 0:
+                left, right = hid[us[0] // TILE], ffw[us[0] : us[0] + TILE, cols(t)]
+            else:
+                left = jnp.concatenate([hid[u // TILE, :, u % TILE : u % TILE + half] for u in us], axis=1)
+                right = jnp.concatenate([ffw[u : u + half, cols(t)] for u in us], axis=0)
+            acc += dot(left, right)
+        return acc
+
+    if ready:
+        for d in far:
+            for p in range(4):
+                pass_on[d][p, 2].wait_recv()
+            pass_on[d][0, 3].wait_recv()
+
+        @pl.loop(0, tiles)
+        def _(t):
+            f1[:, cols(t)] = contract(t, f1[:, cols(t)], ready)
+
     relay("5")
     for d in far:
         for p in range(4):
-            pass_on[d][p, 2].wait_recv()
-            pass_on[d][p, 3].wait_recv()
+            if not ready:
+                pass_on[d][p, 2].wait_recv()
+            if p > 0 or not ready:
+                pass_on[d][p, 3].wait_recv()
 
     @pl.loop(0, tiles)
     def _(t):
-        acc = f1[:, cols(t)]
-        for c in range(2 * per, chunks):
-            acc += dot(hid[c], ffw[c * TILE : (c + 1) * TILE, cols(t)])
-        f1[:, cols(t)] = acc
+        f1[:, cols(t)] = contract(t, f1[:, cols(t)], late)
 
     c_cot.wait()
     cs[...] = jnp.zeros_like(cs)
 
-    @pl.loop(0, rows // BLOCK)
+    @pl.loop(0, rows // BLOCK, unroll=2)
     def _(i):
         r = cols(i, BLOCK)
-        pos = lax.broadcasted_iota(jnp.int32, (BLOCK, width), 0) + i * BLOCK
-        keep = (pos > 0) & (pos < length) & (pos != sep0) & (pos != sep1)
+        pos = lax.broadcasted_iota(jnp.int32, (BLOCK, 1), 0) + i * BLOCK
+        keep = ((pos > 0) & (pos < length) & (pos != sep0) & (pos != sep1)).astype(F32)
         x = f0[r, :] * small[5:6, :] + small[6:7, :] + f1[r, :] + small[7:8, :]
         x = x - mean_rows(x)
         scale = lax.rsqrt(mean_rows(x * x) + eps_norm)
         normed = x * scale
         act[r, :] = (normed * small[8:9, :] + small[9:10, :]).astype(BF16)
-        g = jnp.where(keep, cotb[r, :].astype(F32), 0.0)
+        g = cotb[r, :].astype(F32) * keep
         s = g * small[8:9, :]
         gs = scale * (s - mean_rows(s) - normed * mean_rows(s * normed))
         low = gs.astype(BF16)
@@ -373,7 +404,7 @@
 
     c_act = load(5, act, act_out)
 
-    @pl.loop(0, chunks)
+    @pl.loop(0, chunks, unroll=2)
     def _(c):
         gi = (dot_nt(a1[...], ffw[cols(c), :]) * slope[c]).astype(BF16)
         hid[c] = gi
@@ -388,7 +419,7 @@
             acc += dot_nt(hid[c], inw[c, cols(t), :])
         f1[:, cols(t)] = acc
 
-    @pl.loop(0, rows // BLOCK)
+    @pl.loop(0, rows // BLOCK, unroll=2)
     def _(i):
         r = cols(i, BLOCK)
         g = f1[r, :] + f2[r, :]
@@ -475,19 +506,18 @@
     for c in t_sum + t_inb:
         c.start()
 
-    @pl.loop(0, tiles)
+    @pl.loop(0, tiles, unroll=2)
     def _(n):
         a1[:, cols(n)] = dot_nt(a0[...], outw[cols(n), :]).astype(BF16)
 
     @pl.loop(0, tiles)
     def _(n):
         kt = k[n].T
-        dqs, dks, dvs = [], [], []
+        dqs, dvs = [], []
         for p in range(TILE // LANES):
             v2 = v[n, :, p * LANES : (p + 1) * LANES]
-            qs = halves(q[n, :, p * LANES : (p + 1) * LANES])
             gs = halves(a1[:, cols(2 * n + p, LANES)])
-            dk, dv = None, None
+            dv = None
             for e in range(2):
                 h = 2 * p + e
                 dprob = dot_nt(v2, gs[e])
@@ -496,47 +526,49 @@
                 t = prob * dprob
                 ds = (t - prob * jnp.sum(t, axis=0, keepdims=True)).astype(BF16)
                 dvh = dot(low, gs[e])
-                dkh = dot(ds, qs[e])
+                pt[n * heads + h] = ds
                 dv = dvh if dv is None else dv + dvh
-                dk = dkh if dk is None else dk + dkh
                 dqs.append(dot(kt[h * hd : (h + 1) * hd], ds))
-            dks.append(dk)
             dvs.append(dv)
         dq = (jnp.concatenate(dqs, axis=0) * hd**-0.5).astype(BF16).T
         dv = jnp.concatenate(dvs, axis=1).astype(BF16)
-        q[n] = dq
-        k[n] = jnp.concatenate(dks, axis=1).astype(BF16)
+        hid[n] = dq
         v[n] = dv
         csqv[0, :, cols(n)] = fold8(dq.astype(F32))
         csqv[1, :, cols(n)] = fold8(dv.astype(F32))
-        for s in range(min(steps, tiles)):
-
-            @pl.when(n == s)
+        for s, at in ((0, 0), (1, tiles - 1)):
+
+            @pl.when(n == at)
             def _(s=s):
                 reduce_sums(s)
 
-    for s in range(tiles, steps):
+    for s in range(2, steps):
         reduce_sums(s)
     for i in range(2):
         tqv[0, i : i + 1, :] = total8(csqv[i])
     for c in t_qv:
         c.start()
 
-    @pl.loop(0, tiles)
+    @pl.loop(0, tiles, unroll=2)
+    def _(n):
+        dks = []
+        for p in range(TILE // LANES):
+            lo, hi = halves(q[n, :, p * LANES : (p + 1) * LANES])
+            dks.append(dot(pt[n * heads + 2 * p], lo) + dot(pt[n * heads + 2 * p + 1], hi))
+        k[n] = jnp.concatenate(dks, axis=1).astype(BF16)
+
+    reduce_qv(0)
+
+    @pl.loop(0, tiles, unroll=2)
     def _(t):
         acc = f2[:, cols(t)]
         for n in range(tiles):
-            for i, ref in enumerate((q, k, v)):
+            for i, ref in enumerate((hid, k, v)):
                 acc += dot_nt(ref[n], qkvw[n + i * tiles, cols(t), :])
         f1[:, cols(t)] = acc
-        for s in range(min(steps, tiles - 1)):
-
-            @pl.when(t == s + 1)
-            def _(s=s):
-                reduce_qv(s)
-
-    c_grad = load(6, f1, grad_out)
-    for s in range(min(steps, tiles - 1), steps):
+        pltpu.make_async_copy(f1.at[:, cols(t)], grad_out.at[:, cols(t)], lsem.at[20 + t]).start()
+
+    for s in range(1, steps):
         reduce_qv(s)
     last = near + 2 * (steps - 2)
     outs = [load(7, sbuf.at[last], sums_out), load(16, qbuf.at[last], qv_out), load(17, ibuf.at[last], inb_out)]
@@ -546,7 +578,8 @@
             c.wait_send()
     for c in core_in + [core_ffn] + bias + t_sum + t_inb + t_qv + sum(d_sum + d_inb + d_qv, []):
         c.wait_send()
-    for c in [c_act, c_grad] + outs:
+    c_grad = [pltpu.make_async_copy(f1.at[:, cols(t)], grad_out.at[:, cols(t)], lsem.at[20 + t]) for t in range(tiles)]
+    for c in [c_act] + c_grad + outs:
         c.wait()
     assert count[0] <= send.shape[0]
 
@@ -594,7 +627,6 @@
     vectors = (type_table, qv_bias, out_bias, gain_one, shift_one, ffn_bias, gain_two, shift_two)
     V = pltpu.VMEM
     outside = pl.BlockSpec(memory_space=pl.ANY)
-    scalar = pl.BlockSpec(memory_space=pltpu.SMEM)
     act, grad, sums, qv, inb = pl.pallas_call(
         functools.partial(kernel, ranks, group),
         out_shape=(
@@ -604,7 +636,7 @@
             jax.ShapeDtypeStruct((2, width), F32),
             jax.ShapeDtypeStruct((brow, 1, LANES), F32),
         ),
-        in_specs=[scalar, scalar] + [outside] * 15,
+        in_specs=[outside] * 17,
         out_specs=(outside,) * 5,
         scratch_shapes=[
             V((3 * tiles, width, TILE), BF16),
@@ -639,8 +671,10 @@
             V((slots, 2, width), F32),
             [V(x.shape, x.dtype) for x in vectors],
             [V((units,), BF16)] * group,
+            pltpu.SMEM((1,), jnp.int32),
+            pltpu.SMEM((1, 2), jnp.int32),
             pltpu.SemaphoreType.DMA((3 * tiles + units // TILE,)),
-            pltpu.SemaphoreType.DMA((18,)),
+            pltpu.SemaphoreType.DMA((20 + tiles,)),
             pltpu.SemaphoreType.DMA((copies,)),
             pltpu.SemaphoreType.DMA((copies,)),
         ],

time: 97.6 us -> 91.7 us (0.940)
  Pallas kernels: 96 us -> 90 us
    pallas_call x1, Pallas kernels: 93 us -> 87 us  [step(): pl.pallas_call(functools.partial(kernel, ranks, group), out_shape=(jax.Sh...]
where the time goes in v4:
time: 91.7 us; the launch traced here: 91.4 us
  Pallas kernels  90 us (98%)
  between operations  1.45 us (2%)
    pallas_call x1, Pallas kernels, step(): pl.pallas_call(functools.partial(kernel, ranks, group), out_shape=(jax.Sh...  87 us
    pallas_call x1, Pallas kernels, step(): pl.pallas_call(finish, out_shape=(jax.ShapeDtypeStruct((rows, width), BF1...  3.01 us

profile of v4, /device:TPU:0, one launch (start us, length us, event | category | flops | bytes accessed | tf_op | source)
XLA Modules:
  0.0 91.4 jit_solution(6113810296527296335)
XLA Ops:
  1.3 87.0 %shard_map.224 = (bf16[512,1024]{1,0:T(8,128)(2,1)}, f32[512,1024]{1,0:T(8,128)}, f32[4,1024]{1,0:T(4,128)}, f32[2,1024]{1,0:T(2,128)}, f32[8,1,128]{2,1,0:T(1,128)}) custom-call(s32[1]{0:T(128)S(6)} %copy.25.lengths, s32[1,2]{1,0:T(1,128)} %separators.1, bf16[2,1024]{1,0:T(2,128)(2,1)} %table.1, bf16[2,1024]{1,0:T(2,128)(2,1)} %qv_b.1, ...), custom_call_target="tpu_custom_call" | custom-call | tf_op jit(solution)/shard_map/pallas_call | solution.py:630
  88.2 3.0 %shard_map.225 = (bf16[512,1024]{1,0:T(8,128)(2,1)}, f32[512,1024]{1,0:T(8,128)}, f32[2,1024]{1,0:T(2,128)}, f32[1,1024]{1,0:T(1,128)}, f32[1,1024]{1,0:T(1,128)...) custom-call(bf16[512,1024]{1,0:T(8,128)(2,1)} %get-tuple-element.21.act, ...), custom_call_target="tpu_custom_call" | custom-call | tf_op jit(solution)/shard_map/pallas_call | solution.py:695

commit v5 on v4

--- a/solution.py
+++ b/solution.py
@@ -53,9 +53,9 @@
     ranks, group,
     lengths, separators, table, qv_b, out_b, gain1, shift1, ffn_b, gain2, shift2, in_b, tokens, cot, qkv_w, out_w, in_w, ffn_w,
     act_out, grad_out, sums_out, qv_out, inb_out,
-    qkvw, outw, inw, ffw, inb, q, k, v, pt, slope, hid, a0, a1, f0, f1, f2, tok, cotb, act, sc1, cs, csqv,
+    qkvw, outw, inw, ffw, inb, q, k, v, pt, slope, hid, a0, a1, f0, f1, f2, tok, cotb, sc1, cs, csqv,
     small, ginb, rinb, ibuf, tsum, sbuf, tqv, qbuf,
-    raw, inraw, len_s, sep_s, wsem, lsem, send, recv,
+    raw, inraw, len_s, sep_s, mask, mixt, wsem, lsem, send, recv,
 ):
     rows, width = tok.shape
     tiles = width // TILE
@@ -99,17 +99,21 @@
     def natural(p):
         return (p + dp) % 2 + (p // 2 + dp // 2) % 2 * 2
 
+    cut = width // 4
+
     def piece(slot, p, i):
         u = slot * units + p * part
-        if i < 2:
-            return inw.at[u // TILE, pl.ds(i * width // 2, width // 2), pl.ds(u % TILE, part)]
-        return ffw.at[pl.ds(u + (i - 2) * part // 2, part // 2), :]
+        if i == "in":
+            return inw.at[u // TILE, :, pl.ds(u % TILE, part)]
+        if i < 4:
+            return inw.at[u // TILE, pl.ds(i * cut, cut), pl.ds(u % TILE, part)]
+        return ffw.at[pl.ds(u + (i - 4) * part // 2, part // 2), :]
 
     def source(p, i):
         u = pl.multiple_of(natural(p) * part, part)
-        if i < 2:
-            return in_w.at[pl.ds(i * width // 2, width // 2), pl.ds(u, part)]
-        return ffn_w.at[pl.ds(u + (i - 2) * part // 2, part // 2), :]
+        if i < 4:
+            return in_w.at[pl.ds(i * cut, cut), pl.ds(u, part)]
+        return ffn_w.at[pl.ds(u + (i - 4) * part // 2, part // 2), :]
 
     def load(i, src, dst):
         c = pltpu.make_async_copy(src, dst, lsem.at[i])
@@ -135,10 +139,11 @@
     c_cot = load(4, cot, cotb)
 
     far = range(1, line)
-    direct = {d: [remote(source(p, i), piece(2 * d, p, i), place(-d, 0)) for p, i in ((0, 0), (0, 1), (0, 2), (0, 3), (3, 2), (3, 3))] for d in far}
-    to_x = {d: [remote(piece(2 * d, p, i), piece(2 * d, p + 1, i), rank(1)) for p, i in ((0, 0), (0, 1), (0, 2), (0, 3), (2, 0))] for d in far}
-    to_z = {d: [remote(piece(2 * d, p, i), piece(2 * d, p + 2, i), rank(2)) for p, i in ((0, 0), (0, 1), (0, 2), (0, 3), (1, 1))] for d in far}
-    pass_on = {d: {(p, i): remote(piece(2 * d, p, i), piece(2 * d + 1, p, i), place(0, 1)) for p in range(4) for i in range(4)} for d in far}
+    near_pieces = [(0, i) for i in range(6)]
+    direct = {d: [remote(source(p, i), piece(2 * d, p, i), place(-d, 0)) for p, i in near_pieces + [(3, 4), (3, 5)]] for d in far}
+    to_x = {d: [remote(piece(2 * d, p, i), piece(2 * d, p + 1, i), rank(1)) for p, i in near_pieces + [(2, 0), (2, 1)]] for d in far}
+    to_z = {d: [remote(piece(2 * d, p, i), piece(2 * d, p + 2, i), rank(2)) for p, i in near_pieces + [(1, 2), (1, 3)]] for d in far}
+    pass_on = {d: {(p, i): remote(piece(2 * d, p, i), piece(2 * d + 1, p, i), place(0, 1)) for p in range(4) for i in ("in", 4, 5)} for d in far}
     core_in = [remote(in_w.at[:, n * TILE : (n + 1) * TILE], inw.at[per + n], place(0, 1)) for n in range(per)]
     core_ffn = remote(ffn_w, ffw.at[pl.ds(units, units), :], place(0, 1))
     bias = [remote(in_b, inraw[s], place(-(s // 2), s % 2)) for s in range(1, group)]
@@ -146,37 +151,39 @@
     def relay(step):
         for d in far:
             yd, xd, zd, on = direct[d], to_x[d], to_z[d], pass_on[d]
-            if step in ("0", "1", "2", "3"):
-                i = int(step)
-                yd[i].wait_recv()
-                xd[i].start()
-                zd[i].start()
-                on[0, i].start()
-            if step == "in0":
+            if step in range(6):
+                yd[step].wait_recv()
+                xd[step].start()
+                zd[step].start()
+                if step >= 3:
+                    on[0, "in" if step == 3 else step].start()
+            if step == "dx":
                 zd[0].wait_recv()
-                xd[4].start()
-                on[2, 0].start()
-                xd[0].wait_recv()
-                on[1, 0].start()
-            if step == "in1":
-                xd[1].wait_recv()
-                zd[4].start()
-                on[1, 1].start()
                 zd[1].wait_recv()
-                on[2, 1].start()
-            if step == "in":
-                xd[4].wait_recv()
-                on[3, 0].start()
-                zd[4].wait_recv()
-                on[3, 1].start()
-            if step in ("4", "5"):
-                i = int(step)
-                yd[i].wait_recv()
-                on[3, i - 2].start()
-                xd[i - 2].wait_recv()
-                on[1, i - 2].start()
-                zd[i - 2].wait_recv()
-                on[2, i - 2].start()
+                xd[6].start()
+                xd[7].start()
+            if step == "dz":
+                for i in range(4):
+                    xd[i].wait_recv()
+                zd[6].start()
+                zd[7].start()
+                on[1, "in"].start()
+                zd[2].wait_recv()
+                zd[3].wait_recv()
+                on[2, "in"].start()
+            if step == "diag":
+                for i in (6, 7):
+                    xd[i].wait_recv()
+                    zd[i].wait_recv()
+                on[3, "in"].start()
+            if step in ("f4", "f5"):
+                i = int(step[1])
+                yd[i + 2].wait_recv()
+                on[3, i].start()
+                xd[i].wait_recv()
+                on[1, i].start()
+                zd[i].wait_recv()
+                on[2, i].start()
 
     pl.semaphore_wait(barrier, len(friends))
     for c in bias:
@@ -220,6 +227,7 @@
     def _(n):
         k[n] = dot(a0[...], qkvw[n + tiles]).astype(BF16)
 
+    relay(0)
     for c in c_qkv[2 * tiles :]:
         c.wait()
 
@@ -227,8 +235,7 @@
     def _(n):
         v[n] = (dot(a0[...], qkvw[n + 2 * tiles]) + small[3:4, cols(n)]).astype(BF16)
 
-    relay("0")
-
+    mask[...] = jnp.where(lax.broadcasted_iota(jnp.int32, (rows, LANES), 0) < length, 0.0, -1e30)
     low_half = lax.broadcasted_iota(jnp.int32, (rows, LANES), 1) < hd
     zero = jnp.zeros((rows, LANES), BF16)
     heads = TILE // hd
@@ -239,30 +246,26 @@
     @pl.loop(0, tiles)
     def _(n):
         vt = v[n].T
-        outs = []
-        for p in range(TILE // LANES):
-            k2 = k[n, :, p * LANES : (p + 1) * LANES]
-            for e, qm in enumerate(halves(q[n, :, p * LANES : (p + 1) * LANES])):
-                h = 2 * p + e
-                s = dot_nt(k2, qm)
-                kpos = lax.broadcasted_iota(jnp.int32, s.shape, 0)
-                s = jnp.where(kpos < length, s, -1e30)
-                top = jnp.max(s, axis=0, keepdims=True)
-                ex = jnp.exp(s - top)
-                prob = (ex * (1.0 / jnp.sum(ex, axis=0, keepdims=True))).astype(BF16)
-                pt[n * heads + h] = prob
-                outs.append(dot(vt[h * hd : (h + 1) * hd], prob))
-        a1[:, cols(n)] = jnp.concatenate(outs, axis=0).astype(BF16).T
-
-        @pl.when(n == 1)
-        def _():
-            relay("1")
-
-        @pl.when(n == 2)
-        def _():
-            relay("in0")
-
-    relay("2")
+        hide = jnp.concatenate([mask[...]] * (rows // LANES), axis=1)
+        pairs = [(k[n, :, p * LANES : (p + 1) * LANES], qm) for p in range(TILE // LANES) for qm in halves(q[n, :, p * LANES : (p + 1) * LANES])]
+        scores = [dot_nt(*pairs[0])]
+        for h in range(heads):
+            if h + 1 < heads:
+                scores.append(dot_nt(*pairs[h + 1]))
+            s = scores[h] + hide
+            ex = jnp.exp(s - jnp.max(s, axis=0, keepdims=True))
+            prob = (ex * (1.0 / jnp.sum(ex, axis=0, keepdims=True))).astype(BF16)
+            pt[n * heads + h] = prob
+            mixt[n, h * hd : (h + 1) * hd] = dot(vt[h * hd : (h + 1) * hd], prob)
+        a1[:, cols(n)] = mixt[n].astype(BF16).T
+
+        for i, at in enumerate((0, 1, 2)):
+
+            @pl.when(n == at)
+            def _(i=i):
+                relay(i + 1)
+
+    relay("dx")
 
     c_out.wait()
 
@@ -270,6 +273,7 @@
     def _(n):
         f1[:, cols(n)] = dot(a1[...], outw[:, cols(n)]) + small[4:5, cols(n)] + f0[:, cols(n)]
 
+    relay("dz")
 
     @pl.loop(0, rows // BLOCK, unroll=2)
     def _(i):
@@ -282,7 +286,7 @@
         a0[r, :] = (normed * small[5:6, :] + small[6:7, :]).astype(BF16)
         sc1[r, :] = jnp.broadcast_to(scale, (BLOCK, LANES))
 
-    relay("in1")
+    relay(4)
 
     def hidden_units(c, first, second):
         x = dot(a0[...], inw[c]) + jnp.concatenate([inb[first], inb[second]], axis=1)
@@ -299,13 +303,9 @@
         for r in range(brow):
             inb[t * brow + r] = b[:, r * LANES : (r + 1) * LANES]
 
-    @pl.loop(0, 2 * per)
+    @pl.loop(0, 2 * per, unroll=2)
     def _(c):
         hidden_units(c, 2 * c, 2 * c + 1)
-
-        @pl.when(c == 2 * per - 4)
-        def _():
-            relay("3")
 
     def shuffled(r):
         return r // brow * brow + natural(r % brow // prow) * prow + r % prow
@@ -314,18 +314,19 @@
         for d in far:
             for p in range(4):
                 if (p * part) // TILE == i:
-                    pass_on[d][p, 0].wait_recv()
-                    pass_on[d][p, 1].wait_recv()
-
-        @pl.loop(2, group)
+                    pass_on[d][p, "in"].wait_recv()
+
+        @pl.loop(2, group, unroll=2)
         def _(t):
             c = t * per + i
             hidden_units(c, shuffled(2 * c), shuffled(2 * c + 1))
 
-    early = per - 1
-    for i in range(early):
+    units_of(0)
+    relay(5)
+    for i in range(1, per):
+        if i == per - 2 or per == 2:
+            relay("diag")
         units_of(i)
-    relay("in")
     c_ffn.wait()
     core_ffn.wait_recv()
 
@@ -336,9 +337,10 @@
             acc += dot(hid[c], ffw[c * TILE : (c + 1) * TILE, cols(t)])
         f1[:, cols(t)] = acc
 
-    relay("4")
-    for i in range(early, per):
-        units_of(i)
+        @pl.when(t == tiles - 2)
+        def _():
+            relay("f4")
+
     half = part // 2
     blocks = [(t * units + p * part + h * half, h > 0 and p > 0) for t in range(2, group) for p in range(4) for h in range(2)]
     if half % LANES:
@@ -361,20 +363,20 @@
     if ready:
         for d in far:
             for p in range(4):
-                pass_on[d][p, 2].wait_recv()
-            pass_on[d][0, 3].wait_recv()
+                pass_on[d][p, 4].wait_recv()
+            pass_on[d][0, 5].wait_recv()
 
         @pl.loop(0, tiles)
         def _(t):
             f1[:, cols(t)] = contract(t, f1[:, cols(t)], ready)
 
-    relay("5")
+    relay("f5")
     for d in far:
         for p in range(4):
             if not ready:
-                pass_on[d][p, 2].wait_recv()
+                pass_on[d][p, 4].wait_recv()
             if p > 0 or not ready:
-                pass_on[d][p, 3].wait_recv()
+                pass_on[d][p, 5].wait_recv()
 
     @pl.loop(0, tiles)
     def _(t):
@@ -392,7 +394,7 @@
         x = x - mean_rows(x)
         scale = lax.rsqrt(mean_rows(x * x) + eps_norm)
         normed = x * scale
-        act[r, :] = (normed * small[8:9, :] + small[9:10, :]).astype(BF16)
+        tok[r, :] = (normed * small[8:9, :] + small[9:10, :]).astype(BF16)
         g = cotb[r, :].astype(F32) * keep
         s = g * small[8:9, :]
         gs = scale * (s - mean_rows(s) - normed * mean_rows(s * normed))
@@ -402,7 +404,7 @@
         cs[0] += fold8(g)
         cs[1] += fold8(low.astype(F32))
 
-    c_act = load(5, act, act_out)
+    c_act = load(5, tok, act_out)
 
     @pl.loop(0, chunks, unroll=2)
     def _(c):
@@ -513,37 +515,30 @@
     @pl.loop(0, tiles)
     def _(n):
         kt = k[n].T
-        dqs, dvs = [], []
-        for p in range(TILE // LANES):
-            v2 = v[n, :, p * LANES : (p + 1) * LANES]
-            gs = halves(a1[:, cols(2 * n + p, LANES)])
-            dv = None
-            for e in range(2):
-                h = 2 * p + e
-                dprob = dot_nt(v2, gs[e])
-                low = pt[n * heads + h]
-                prob = low.astype(F32)
-                t = prob * dprob
-                ds = (t - prob * jnp.sum(t, axis=0, keepdims=True)).astype(BF16)
-                dvh = dot(low, gs[e])
-                pt[n * heads + h] = ds
-                dv = dvh if dv is None else dv + dvh
-                dqs.append(dot(kt[h * hd : (h + 1) * hd], ds))
-            dvs.append(dv)
+        gt = a1[:, cols(n)].T.astype(F32)
+        inner = jnp.sum((gt * mixt[n]).reshape(heads, hd, rows), axis=1)
+        pairs = [(v[n, :, p * LANES : (p + 1) * LANES], gm) for p in range(TILE // LANES) for gm in halves(a1[:, cols(2 * n + p, LANES)])]
+        dqs, dvh = [], []
+        dprobs = [dot_nt(*pairs[0])]
+        for h in range(heads):
+            if h + 1 < heads:
+                dprobs.append(dot_nt(*pairs[h + 1]))
+            low = pt[n * heads + h]
+            ds = (low.astype(F32) * (dprobs[h] - inner[h : h + 1])).astype(BF16)
+            dvh.append(dot(low, pairs[h][1]))
+            pt[n * heads + h] = ds
+            dqs.append(dot(kt[h * hd : (h + 1) * hd], ds))
+        dvs = [dvh[2 * p] + dvh[2 * p + 1] for p in range(TILE // LANES)]
         dq = (jnp.concatenate(dqs, axis=0) * hd**-0.5).astype(BF16).T
         dv = jnp.concatenate(dvs, axis=1).astype(BF16)
         hid[n] = dq
         v[n] = dv
         csqv[0, :, cols(n)] = fold8(dq.astype(F32))
         csqv[1, :, cols(n)] = fold8(dv.astype(F32))
-        for s, at in ((0, 0), (1, tiles - 1)):
-
-            @pl.when(n == at)
-            def _(s=s):
-                reduce_sums(s)
-
-    for s in range(2, steps):
-        reduce_sums(s)
+        @pl.when(n == 0)
+        def _():
+            reduce_sums(0)
+
     for i in range(2):
         tqv[0, i : i + 1, :] = total8(csqv[i])
     for c in t_qv:
@@ -569,6 +564,7 @@
         pltpu.make_async_copy(f1.at[:, cols(t)], grad_out.at[:, cols(t)], lsem.at[20 + t]).start()
 
     for s in range(1, steps):
+        reduce_sums(s)
         reduce_qv(s)
     last = near + 2 * (steps - 2)
     outs = [load(7, sbuf.at[last], sums_out), load(16, qbuf.at[last], qv_out), load(17, ibuf.at[last], inb_out)]
@@ -623,7 +619,7 @@
     near = min(ranks, 8)
     far_bits = (ranks // near).bit_length() - 1
     slots = near + 2 * far_bits + 1
-    copies = (line - 1) * 32 + units // TILE + 1 + 4 * (group - 1) + 3 * (near - 1 + far_bits)
+    copies = (line - 1) * 36 + units // TILE + 1 + 4 * (group - 1) + 3 * (near - 1 + far_bits)
     vectors = (type_table, qv_bias, out_bias, gain_one, shift_one, ffn_bias, gain_two, shift_two)
     V = pltpu.VMEM
     outside = pl.BlockSpec(memory_space=pl.ANY)
@@ -657,7 +653,6 @@
             V((rows, width), F32),
             V((rows, width), BF16),
             V((rows, width), BF16),
-            V((rows, width), BF16),
             V((rows, LANES), F32),
             V((4, 8, width), F32),
             V((2, 8, width), F32),
@@ -673,6 +668,8 @@
             [V((units,), BF16)] * group,
             pltpu.SMEM((1,), jnp.int32),
             pltpu.SMEM((1, 2), jnp.int32),
+            V((rows, LANES), F32),
+            V((tiles, TILE, rows), F32),
             pltpu.SemaphoreType.DMA((3 * tiles + units // TILE,)),
             pltpu.SemaphoreType.DMA((20 + tiles,)),
             pltpu.SemaphoreType.DMA((copies,)),

time: 91.7 us -> 85.4 us (0.931)
  Pallas kernels: 90 us -> 83.7 us
    pallas_call x1, Pallas kernels: 87 us -> 80.7 us  [step(): pl.pallas_call(functools.partial(kernel, ranks, group), out_shape=(jax.Sh...]
where the time goes in v5:
time: 85.4 us; the launch traced here: 85.1 us
  Pallas kernels  83.7 us (98%)
  between operations  1.45 us (2%)
    pallas_call x1, Pallas kernels, step(): pl.pallas_call(functools.partial(kernel, ranks, group), out_shape=(jax.Sh...  80.7 us
    pallas_call x1, Pallas kernels, step(): pl.pallas_call(finish, out_shape=(jax.ShapeDtypeStruct((rows, width), BF1...  3.01 us

profile of v5, /device:TPU:0, one launch (start us, length us, event | category | flops | bytes accessed | tf_op | source)
XLA Modules:
  0.0 85.1 jit_solution(16387175599752264839)
XLA Ops:
  1.3 80.7 %shard_map.224 = (bf16[512,1024]{1,0:T(8,128)(2,1)}, f32[512,1024]{1,0:T(8,128)}, f32[4,1024]{1,0:T(4,128)}, f32[2,1024]{1,0:T(2,128)}, f32[8,1,128]{2,1,0:T(1,128)}) custom-call(s32[1]{0:T(128)S(6)} %copy.25.lengths, s32[1,2]{1,0:T(1,128)} %separators.1, bf16[2,1024]{1,0:T(2,128)(2,1)} %table.1, bf16[2,1024]{1,0:T(2,128)(2,1)} %qv_b.1, ...), custom_call_target="tpu_custom_call" | custom-call | tf_op jit(solution)/shard_map/pallas_call | solution.py:626
  82.0 3.0 %shard_map.225 = (bf16[512,1024]{1,0:T(8,128)(2,1)}, f32[512,1024]{1,0:T(8,128)}, f32[2,1024]{1,0:T(2,128)}, f32[1,1024]{1,0:T(1,128)}, f32[1,1024]{1,0:T(1,128)...) custom-call(bf16[512,1024]{1,0:T(8,128)(2,1)} %get-tuple-element.21.act, ...), custom_call_target="tpu_custom_call" | custom-call | tf_op jit(solution)/shard_map/pallas_call | solution.py:692

commit v6 on v5

--- a/solution.py
+++ b/solution.py
@@ -123,20 +123,9 @@
     c_small = [load(8 + i, src, dst) for i, (src, dst) in enumerate(zip((table, qv_b, out_b, gain1, shift1, ffn_b, gain2, shift2), raw))]
     c_tok = load(0, tokens, tok)
     c_small += [load(18, lengths, len_s), load(19, separators, sep_s)]
-    c_qkv = []
-    for n in range(3 * tiles):
-        c = pltpu.make_async_copy(qkv_w.at[:, n * TILE : (n + 1) * TILE], qkvw.at[n], wsem.at[n])
-        c.start()
-        c_qkv.append(c)
-    c_in = []
-    for n in range(per):
-        c = pltpu.make_async_copy(in_w.at[:, n * TILE : (n + 1) * TILE], inw.at[n], wsem.at[3 * tiles + n])
-        c.start()
-        c_in.append(c)
-    c_out = load(1, out_w, outw)
-    c_ffn = load(2, ffn_w, ffw.at[pl.ds(0, units), :])
-    c_b = load(3, in_b, inraw[0])
-    c_cot = load(4, cot, cotb)
+    c_qkv = [pltpu.make_async_copy(qkv_w.at[:, n * TILE : (n + 1) * TILE], qkvw.at[n], wsem.at[n]) for n in range(3 * tiles)]
+    for c in c_qkv[:tiles]:
+        c.start()
 
     far = range(1, line)
     near_pieces = [(0, i) for i in range(6)]
@@ -191,8 +180,17 @@
     for d in far:
         for c in direct[d]:
             c.start()
+    for c in c_qkv[tiles:]:
+        c.start()
     for c in core_in + [core_ffn]:
         c.start()
+    c_out = load(1, out_w, outw)
+    c_in = [pltpu.make_async_copy(in_w.at[:, n * TILE : (n + 1) * TILE], inw.at[n], wsem.at[3 * tiles + n]) for n in range(per)]
+    for c in c_in:
+        c.start()
+    c_b = load(3, in_b, inraw[0])
+    c_ffn = load(2, ffn_w, ffw.at[pl.ds(0, units), :])
+    c_cot = load(4, cot, cotb)
 
     for c in c_small:
         c.wait()
@@ -323,10 +321,9 @@
 
     units_of(0)
     relay(5)
-    for i in range(1, per):
-        if i == per - 2 or per == 2:
-            relay("diag")
+    for i in range(1, per - 1):
         units_of(i)
+    relay("diag")
     c_ffn.wait()
     core_ffn.wait_recv()
 
@@ -337,16 +334,19 @@
             acc += dot(hid[c], ffw[c * TILE : (c + 1) * TILE, cols(t)])
         f1[:, cols(t)] = acc
 
-        @pl.when(t == tiles - 2)
-        def _():
-            relay("f4")
+    units_of(per - 1)
+    relay("f4")
 
     half = part // 2
-    blocks = [(t * units + p * part + h * half, h > 0 and p > 0) for t in range(2, group) for p in range(4) for h in range(2)]
-    if half % LANES:
-        ready, late = [], [u for u, _ in blocks]
-    else:
-        ready, late = [u for u, last in blocks if not last], [u for u, last in blocks if last]
+    blocks = [(t, p, h, t * units + p * part + h * half) for t in range(2, group) for p in range(4) for h in range(2)]
+
+    def phase(t, p, h):
+        if half % LANES:
+            return 2
+        passed = t % 2 if p else 0
+        return passed + (h if p else 0)
+
+    waves = [[u for t, p, h, u in blocks if phase(t, p, h) == w] for w in range(3)]
 
     def contract(t, acc, starts):
         step = max(1, TILE // half)
@@ -360,32 +360,31 @@
             acc += dot(left, right)
         return acc
 
-    if ready:
-        for d in far:
-            for p in range(4):
-                pass_on[d][p, 4].wait_recv()
-            pass_on[d][0, 5].wait_recv()
-
-        @pl.loop(0, tiles)
-        def _(t):
-            f1[:, cols(t)] = contract(t, f1[:, cols(t)], ready)
-
+    def add_wave(starts):
+        if starts:
+
+            @pl.loop(0, tiles)
+            def _(t):
+                f1[:, cols(t)] = contract(t, f1[:, cols(t)], starts)
+
+    for d in far:
+        pass_on[d][0, 4].wait_recv()
+        pass_on[d][0, 5].wait_recv()
+    add_wave(waves[0])
     relay("f5")
     for d in far:
-        for p in range(4):
-            if not ready:
-                pass_on[d][p, 4].wait_recv()
-            if p > 0 or not ready:
-                pass_on[d][p, 5].wait_recv()
-
-    @pl.loop(0, tiles)
-    def _(t):
-        f1[:, cols(t)] = contract(t, f1[:, cols(t)], late)
+        for p in range(1, 4):
+            pass_on[d][p, 4].wait_recv()
+    add_wave(waves[1])
+    for d in far:
+        for p in range(1, 4):
+            pass_on[d][p, 5].wait_recv()
+    add_wave(waves[2])
 
     c_cot.wait()
     cs[...] = jnp.zeros_like(cs)
 
-    @pl.loop(0, rows // BLOCK, unroll=2)
+    @pl.loop(0, rows // BLOCK, unroll=4)
     def _(i):
         r = cols(i, BLOCK)
         pos = lax.broadcasted_iota(jnp.int32, (BLOCK, 1), 0) + i * BLOCK
@@ -406,7 +405,7 @@
 
     c_act = load(5, tok, act_out)
 
-    @pl.loop(0, chunks, unroll=2)
+    @pl.loop(0, chunks, unroll=4)
     def _(c):
         gi = (dot_nt(a1[...], ffw[cols(c), :]) * slope[c]).astype(BF16)
         hid[c] = gi
@@ -421,7 +420,7 @@
             acc += dot_nt(hid[c], inw[c, cols(t), :])
         f1[:, cols(t)] = acc
 
-    @pl.loop(0, rows // BLOCK, unroll=2)
+    @pl.loop(0, rows // BLOCK, unroll=4)
     def _(i):
         r = cols(i, BLOCK)
         g = f1[r, :] + f2[r, :]

time: 85.4 us -> 82.4 us (0.965)
  Pallas kernels: 83.7 us -> 80.6 us
    pallas_call x1, Pallas kernels: 80.7 us -> 77.6 us  [step(): pl.pallas_call(functools.partial(kernel, ranks, group), out_shape=(jax.Sh...]
where the time goes in v6:
time: 82.4 us; the launch traced here: 82.1 us
  Pallas kernels  80.6 us (98%)
  between operations  1.45 us (2%)
    pallas_call x1, Pallas kernels, step(): pl.pallas_call(functools.partial(kernel, ranks, group), out_shape=(jax.Sh...  77.6 us
    pallas_call x1, Pallas kernels, step(): pl.pallas_call(finish, out_shape=(jax.ShapeDtypeStruct((rows, width), BF1...  3.01 us

profile of v6, /device:TPU:0, one launch (start us, length us, event | category | flops | bytes accessed | tf_op | source)
XLA Modules:
  0.0 82.1 jit_solution(14210014619167771960)
XLA Ops:
  1.3 77.6 %shard_map.224 = (bf16[512,1024]{1,0:T(8,128)(2,1)}, f32[512,1024]{1,0:T(8,128)}, f32[4,1024]{1,0:T(4,128)}, f32[2,1024]{1,0:T(2,128)}, f32[8,1,128]{2,1,0:T(1,128)}) custom-call(s32[1]{0:T(128)S(6)} %copy.25.lengths, s32[1,2]{1,0:T(1,128)} %separators.1, bf16[2,1024]{1,0:T(2,128)(2,1)} %table.1, bf16[2,1024]{1,0:T(2,128)(2,1)} %qv_b.1, ...), custom_call_target="tpu_custom_call" | custom-call | tf_op jit(solution)/shard_map/pallas_call | solution.py:625
  78.9 3.0 %shard_map.225 = (bf16[512,1024]{1,0:T(8,128)(2,1)}, f32[512,1024]{1,0:T(8,128)}, f32[2,1024]{1,0:T(2,128)}, f32[1,1024]{1,0:T(1,128)}, f32[1,1024]{1,0:T(1,128)...) custom-call(bf16[512,1024]{1,0:T(8,128)(2,1)} %get-tuple-element.21.act, ...), custom_call_target="tpu_custom_call" | custom-call | tf_op jit(solution)/shard_map/pallas_call | solution.py:691

commit v7 on v6

--- a/solution.py
+++ b/solution.py
@@ -225,13 +225,20 @@
     def _(n):
         k[n] = dot(a0[...], qkvw[n + tiles]).astype(BF16)
 
-    relay(0)
+    @pl.when(core == 1)
+    def _():
+        relay(0)
+
     for c in c_qkv[2 * tiles :]:
         c.wait()
 
     @pl.loop(0, tiles, unroll=2)
     def _(n):
         v[n] = (dot(a0[...], qkvw[n + 2 * tiles]) + small[3:4, cols(n)]).astype(BF16)
+
+    @pl.when(core == 0)
+    def _():
+        relay(0)
 
     mask[...] = jnp.where(lax.broadcasted_iota(jnp.int32, (rows, LANES), 0) < length, 0.0, -1e30)
     low_half = lax.broadcasted_iota(jnp.int32, (rows, LANES), 1) < hd
@@ -342,11 +349,10 @@
 
     def phase(t, p, h):
         if half % LANES:
-            return 2
-        passed = t % 2 if p else 0
-        return passed + (h if p else 0)
-
-    waves = [[u for t, p, h, u in blocks if phase(t, p, h) == w] for w in range(3)]
+            return 3
+        return 2 * h + t % 2 if p else 0
+
+    waves = [[u for t, p, h, u in blocks if phase(t, p, h) == w] for w in range(4)]
 
     def contract(t, acc, starts):
         step = max(1, TILE // half)
@@ -363,7 +369,7 @@
     def add_wave(starts):
         if starts:
 
-            @pl.loop(0, tiles)
+            @pl.loop(0, tiles, unroll=2)
             def _(t):
                 f1[:, cols(t)] = contract(t, f1[:, cols(t)], starts)
 
@@ -371,15 +377,16 @@
         pass_on[d][0, 4].wait_recv()
         pass_on[d][0, 5].wait_recv()
     add_wave(waves[0])
-    relay("f5")
     for d in far:
         for p in range(1, 4):
             pass_on[d][p, 4].wait_recv()
     add_wave(waves[1])
+    relay("f5")
+    add_wave(waves[2])
     for d in far:
         for p in range(1, 4):
             pass_on[d][p, 5].wait_recv()
-    add_wave(waves[2])
+    add_wave(waves[3])
 
     c_cot.wait()
     cs[...] = jnp.zeros_like(cs)
@@ -405,7 +412,7 @@
 
     c_act = load(5, tok, act_out)
 
-    @pl.loop(0, chunks, unroll=4)
+    @pl.loop(0, chunks, unroll=8)
     def _(c):
         gi = (dot_nt(a1[...], ffw[cols(c), :]) * slope[c]).astype(BF16)
         hid[c] = gi
@@ -543,7 +550,7 @@
     for c in t_qv:
         c.start()
 
-    @pl.loop(0, tiles, unroll=2)
+    @pl.loop(0, tiles, unroll=4)
     def _(n):
         dks = []
         for p in range(TILE // LANES):
@@ -553,7 +560,7 @@
 
     reduce_qv(0)
 
-    @pl.loop(0, tiles, unroll=2)
+    @pl.loop(0, tiles, unroll=4)
     def _(t):
         acc = f2[:, cols(t)]
         for n in range(tiles):

time: 82.4 us -> 81.4 us (0.988)
  Pallas kernels: 80.6 us -> 79.5 us
    pallas_call x1, Pallas kernels: 77.6 us -> 76.5 us  [step(): pl.pallas_call(functools.partial(kernel, ranks, group), out_shape=(jax.Sh...]
where the time goes in v7:
time: 81.4 us; the launch traced here: 80.9 us
  Pallas kernels  79.5 us (98%)
  between operations  1.45 us (2%)
    pallas_call x1, Pallas kernels, step(): pl.pallas_call(functools.partial(kernel, ranks, group), out_shape=(jax.Sh...  76.5 us
    pallas_call x1, Pallas kernels, step(): pl.pallas_call(finish, out_shape=(jax.ShapeDtypeStruct((rows, width), BF1...  3.01 us

profile of v7, /device:TPU:0, one launch (start us, length us, event | category | flops | bytes accessed | tf_op | source)
XLA Modules:
  0.0 80.9 jit_solution(1714251377299164194)
XLA Ops:
  1.3 76.5 %shard_map.224 = (bf16[512,1024]{1,0:T(8,128)(2,1)}, f32[512,1024]{1,0:T(8,128)}, f32[4,1024]{1,0:T(4,128)}, f32[2,1024]{1,0:T(2,128)}, f32[8,1,128]{2,1,0:T(1,128)}) custom-call(s32[1]{0:T(128)S(6)} %copy.25.lengths, s32[1,2]{1,0:T(1,128)} %separators.1, bf16[2,1024]{1,0:T(2,128)(2,1)} %table.1, bf16[2,1024]{1,0:T(2,128)(2,1)} %qv_b.1, ...), custom_call_target="tpu_custom_call" | custom-call | tf_op jit(solution)/shard_map/pallas_call | solution.py:632
  77.8 3.0 %shard_map.225 = (bf16[512,1024]{1,0:T(8,128)(2,1)}, f32[512,1024]{1,0:T(8,128)}, f32[2,1024]{1,0:T(2,128)}, f32[1,1024]{1,0:T(1,128)}, f32[1,1024]{1,0:T(1,128)...) custom-call(bf16[512,1024]{1,0:T(8,128)(2,1)} %get-tuple-element.21.act, ...), custom_call_target="tpu_custom_call" | custom-call | tf_op jit(solution)/shard_map/pallas_call | solution.py:698

commit v8 on v7

--- a/solution.py
+++ b/solution.py
@@ -87,14 +87,20 @@
     for f in friends:
         pl.semaphore_signal(barrier, inc=1, device_id=f, device_id_type=MESH)
 
-    count = [0]
-
-    def remote(src, dst, device):
-        i = count[0]
-        count[0] += 1
+    sent, got = {}, {}
+
+    def remote(src, dst, device, out, into):
+        s = sent.setdefault(out, len(sent))
+        r = got.setdefault(into, len(got))
         return pltpu.make_async_remote_copy(
-            src_ref=src, dst_ref=dst, send_sem=send.at[i], recv_sem=recv.at[i], device_id=device, device_id_type=MESH
+            src_ref=src, dst_ref=dst, send_sem=send.at[s], recv_sem=recv.at[r], device_id=device, device_id_type=MESH
         )
+
+    def all_here(name, ref):
+        pltpu.make_async_copy(ref, ref, recv.at[got[name]]).wait()
+
+    def all_gone(name, ref):
+        pltpu.make_async_copy(ref, ref, send.at[sent[name]]).wait()
 
     def natural(p):
         return (p + dp) % 2 + (p // 2 + dp // 2) % 2 * 2
@@ -103,8 +109,11 @@
 
     def piece(slot, p, i):
         u = slot * units + p * part
-        if i == "in":
-            return inw.at[u // TILE, :, pl.ds(u % TILE, part)]
+        if i in ("in", "top", "low"):
+            r = pl.ds(width // 2 if i == "low" else 0, width if i == "in" else width // 2)
+            return inw.at[u // TILE, r, pl.ds(u % TILE, part)]
+        if i == "ffn":
+            return ffw.at[pl.ds(u, part), :]
         if i < 4:
             return inw.at[u // TILE, pl.ds(i * cut, cut), pl.ds(u % TILE, part)]
         return ffw.at[pl.ds(u + (i - 4) * part // 2, part // 2), :]
@@ -115,64 +124,78 @@
             return in_w.at[pl.ds(i * cut, cut), pl.ds(u, part)]
         return ffn_w.at[pl.ds(u + (i - 4) * part // 2, part // 2), :]
 
+    def loaded(i, ref):
+        pltpu.make_async_copy(ref, ref, wsem.at[i]).wait()
+
     def load(i, src, dst):
         c = pltpu.make_async_copy(src, dst, lsem.at[i])
         c.start()
         return c
 
-    c_small = [load(8 + i, src, dst) for i, (src, dst) in enumerate(zip((table, qv_b, out_b, gain1, shift1, ffn_b, gain2, shift2), raw))]
+    c_small = [load(5 + i, src, dst) for i, (src, dst) in enumerate(zip((table, qv_b, out_b, gain1, shift1, ffn_b, gain2, shift2), raw))]
     c_tok = load(0, tokens, tok)
-    c_small += [load(18, lengths, len_s), load(19, separators, sep_s)]
-    c_qkv = [pltpu.make_async_copy(qkv_w.at[:, n * TILE : (n + 1) * TILE], qkvw.at[n], wsem.at[n]) for n in range(3 * tiles)]
+    c_small += [load(13, lengths, len_s), load(14, separators, sep_s)]
+    c_qkv = [pltpu.make_async_copy(qkv_w.at[:, n * TILE : (n + 1) * TILE], qkvw.at[n], wsem.at[n // tiles]) for n in range(3 * tiles)]
     for c in c_qkv[:tiles]:
         c.start()
 
     far = range(1, line)
     near_pieces = [(0, i) for i in range(6)]
-    direct = {d: [remote(source(p, i), piece(2 * d, p, i), place(-d, 0)) for p, i in near_pieces + [(3, 4), (3, 5)]] for d in far}
-    to_x = {d: [remote(piece(2 * d, p, i), piece(2 * d, p + 1, i), rank(1)) for p, i in near_pieces + [(2, 0), (2, 1)]] for d in far}
-    to_z = {d: [remote(piece(2 * d, p, i), piece(2 * d, p + 2, i), rank(2)) for p, i in near_pieces + [(1, 2), (1, 3)]] for d in far}
-    pass_on = {d: {(p, i): remote(piece(2 * d, p, i), piece(2 * d + 1, p, i), place(0, 1)) for p in range(4) for i in ("in", 4, 5)} for d in far}
-    core_in = [remote(in_w.at[:, n * TILE : (n + 1) * TILE], inw.at[per + n], place(0, 1)) for n in range(per)]
-    core_ffn = remote(ffn_w, ffw.at[pl.ds(units, units), :], place(0, 1))
-    bias = [remote(in_b, inraw[s], place(-(s // 2), s % 2)) for s in range(1, group)]
+    direct, to_x, to_z, pass_on = {}, {}, {}, {}
+    for d in far:
+        e = 2 * d
+        direct[d] = [
+            remote(source(p, i), piece(e, p, i), place(-d, 0), "y", ("y", d, p, i)) for p, i in near_pieces + [(3, 4), (3, 5)]
+        ]
+        to_x[d] = [
+            remote(piece(e, p, i), piece(e, p + 1, i), rank(1), "x", ("x", d, p, "in" if i < 4 else i))
+            for p, i in near_pieces + [(2, 0), (2, 1)]
+        ]
+        to_z[d] = [
+            remote(piece(e, p, i), piece(e, p + 2, i), rank(2), "z", ("z", d, p, i if i > 3 else "low" if i > 1 else "top"))
+            for p, i in near_pieces + [(1, 2), (1, 3)]
+        ]
+        for p in range(4):
+            for i in ("in", 4, 5):
+                name = ("on", d, p, "ffn" if p == 0 and i != "in" else i)
+                pass_on[d, p, i] = remote(piece(e, p, i), piece(e + 1, p, i), place(0, 1), "on", name)
+    core_in = [remote(in_w.at[:, n * TILE : (n + 1) * TILE], inw.at[per + n], place(0, 1), "core", "core") for n in range(per)]
+    core_ffn = remote(ffn_w, ffw.at[pl.ds(units, units), :], place(0, 1), "core", "core_ffn")
+    bias = [remote(in_b, inraw[s], place(-(s // 2), s % 2), ("bias", s), ("bias", s)) for s in range(1, group)]
 
     def relay(step):
         for d in far:
-            yd, xd, zd, on = direct[d], to_x[d], to_z[d], pass_on[d]
+            e = 2 * d
+            yd, xd, zd = direct[d], to_x[d], to_z[d]
             if step in range(6):
                 yd[step].wait_recv()
                 xd[step].start()
                 zd[step].start()
                 if step >= 3:
-                    on[0, "in" if step == 3 else step].start()
+                    pass_on[d, 0, "in" if step == 3 else step].start()
             if step == "dx":
-                zd[0].wait_recv()
-                zd[1].wait_recv()
+                all_here(("z", d, 0, "top"), piece(e, 2, "top"))
                 xd[6].start()
                 xd[7].start()
             if step == "dz":
-                for i in range(4):
-                    xd[i].wait_recv()
+                all_here(("x", d, 0, "in"), piece(e, 1, "in"))
                 zd[6].start()
                 zd[7].start()
-                on[1, "in"].start()
-                zd[2].wait_recv()
-                zd[3].wait_recv()
-                on[2, "in"].start()
+                pass_on[d, 1, "in"].start()
+                all_here(("z", d, 0, "low"), piece(e, 2, "low"))
+                pass_on[d, 2, "in"].start()
             if step == "diag":
-                for i in (6, 7):
-                    xd[i].wait_recv()
-                    zd[i].wait_recv()
-                on[3, "in"].start()
+                all_here(("x", d, 2, "in"), piece(e, 3, "top"))
+                all_here(("z", d, 1, "low"), piece(e, 3, "low"))
+                pass_on[d, 3, "in"].start()
             if step in ("f4", "f5"):
                 i = int(step[1])
                 yd[i + 2].wait_recv()
-                on[3, i].start()
+                pass_on[d, 3, i].start()
                 xd[i].wait_recv()
-                on[1, i].start()
+                pass_on[d, 1, i].start()
                 zd[i].wait_recv()
-                on[2, i].start()
+                pass_on[d, 2, i].start()
 
     pl.semaphore_wait(barrier, len(friends))
     for c in bias:
@@ -185,7 +208,7 @@
     for c in core_in + [core_ffn]:
         c.start()
     c_out = load(1, out_w, outw)
-    c_in = [pltpu.make_async_copy(in_w.at[:, n * TILE : (n + 1) * TILE], inw.at[n], wsem.at[3 * tiles + n]) for n in range(per)]
+    c_in = [pltpu.make_async_copy(in_w.at[:, n * TILE : (n + 1) * TILE], inw.at[n], wsem.at[3]) for n in range(per)]
     for c in c_in:
         c.start()
     c_b = load(3, in_b, inraw[0])
@@ -211,15 +234,13 @@
         f0[r, :] = e
         a0[r, :] = e.astype(BF16)
 
-    for c in c_qkv[:tiles]:
-        c.wait()
+    loaded(0, qkvw.at[pl.ds(0, tiles)])
 
     @pl.loop(0, tiles, unroll=2)
     def _(n):
         q[n] = (dot(a0[...], qkvw[n]) + small[2:3, cols(n)]).astype(BF16) * jnp.asarray(hd**-0.5, BF16)
 
-    for c in c_qkv[tiles : 2 * tiles]:
-        c.wait()
+    loaded(1, qkvw.at[pl.ds(tiles, tiles)])
 
     @pl.loop(0, tiles, unroll=2)
     def _(n):
@@ -229,8 +250,7 @@
     def _():
         relay(0)
 
-    for c in c_qkv[2 * tiles :]:
-        c.wait()
+    loaded(2, qkvw.at[pl.ds(2 * tiles, tiles)])
 
     @pl.loop(0, tiles, unroll=2)
     def _(n):
@@ -299,9 +319,10 @@
         hid[c] = (x * cdf).astype(BF16)
         slope[c] = cdf + x * (inv_root_tau * jnp.exp(-0.5 * x * x))
 
-    for c in c_in + [c_b]:
-        c.wait()
-    for c in core_in + bias:
+    loaded(3, inw.at[pl.ds(0, per)])
+    c_b.wait()
+    all_here("core", inw.at[pl.ds(per, per)])
+    for c in bias:
         c.wait_recv()
     for t in range(group):
         b = inraw[t][...].astype(F32).reshape(1, units)
@@ -319,7 +340,7 @@
         for d in far:
             for p in range(4):
                 if (p * part) // TILE == i:
-                    pass_on[d][p, "in"].wait_recv()
+                    pass_on[d, p, "in"].wait_recv()
 
         @pl.loop(2, group, unroll=2)
         def _(t):
@@ -374,18 +395,17 @@
                 f1[:, cols(t)] = contract(t, f1[:, cols(t)], starts)
 
     for d in far:
-        pass_on[d][0, 4].wait_recv()
-        pass_on[d][0, 5].wait_recv()
+        all_here(("on", d, 0, "ffn"), piece(2 * d + 1, 0, "ffn"))
     add_wave(waves[0])
     for d in far:
         for p in range(1, 4):
-            pass_on[d][p, 4].wait_recv()
+            pass_on[d, p, 4].wait_recv()
     add_wave(waves[1])
     relay("f5")
     add_wave(waves[2])
     for d in far:
         for p in range(1, 4):
-            pass_on[d][p, 5].wait_recv()
+            pass_on[d, p, 5].wait_recv()
     add_wave(waves[3])
 
     c_cot.wait()
@@ -410,7 +430,7 @@
         cs[0] += fold8(g)
         cs[1] += fold8(low.astype(F32))
 
-    c_act = load(5, tok, act_out)
+    c_act = load(4, tok, act_out)
 
     @pl.loop(0, chunks, unroll=8)
     def _(c):
@@ -443,20 +463,22 @@
     for i in range(4):
         tsum[0, i : i + 1, :] = total8(cs[i])
     peers = [(s, place(s // 2, s % 2)) for s in range(1, group)]
-    t_sum = [remote(tsum.at[0], tsum.at[s], dev) for s, dev in peers]
-    t_inb = [remote(ginb.at[pl.ds(s * brow, brow)], rinb.at[s], dev) for s, dev in peers]
+    t_sum = [remote(tsum.at[0], tsum.at[s], dev, "t_sum", "t_sum") for s, dev in peers]
+    t_inb = [remote(ginb.at[pl.ds(s * brow, brow)], rinb.at[s], dev, "t_inb", "t_inb") for s, dev in peers]
     hops = [list(range(1, near))] + [[w] for w in wide]
     steps = len(hops) + 1
 
-    def spread(ref):
-        copies, base = [], 0
-        for hop in hops:
-            copies.append([remote(ref.at[base], ref.at[base + i + 1], rank(o)) for i, o in enumerate(hop)])
-            base += len(hop) + 1
-        return copies
-
-    d_sum, d_inb, d_qv = spread(sbuf), spread(ibuf), spread(qbuf)
-    t_qv = [remote(tqv.at[0], tqv.at[s], dev) for s, dev in peers]
+    bases = [0] + [near + 2 * i for i in range(len(wide))]
+
+    def spread(name, ref):
+        return [
+            [remote(ref.at[base], ref.at[base + i + 1], rank(o), (name, base), (name, base)) for i, o in enumerate(hop)]
+            for base, hop in zip(bases, hops)
+        ]
+
+    d_sum, d_inb, d_qv = spread("sum", sbuf), spread("inb", ibuf), spread("qv", qbuf)
+    t_qv = [remote(tqv.at[0], tqv.at[s], dev, "t_qv", "t_qv") for s, dev in peers]
+    others = pl.ds(1, group - 1)
 
     def over_tensor(ref):
         acc = None
@@ -474,14 +496,14 @@
         base = near + 2 * (hop - 1)
         return ref[base] + ref[base + 1]
 
-    def go(step, buffers, copies, totals):
+    def go(step, names, buffers, copies, totals):
         if step == 0:
             for ref, value in zip(buffers, totals()):
                 ref[0] = value
         else:
-            for ref, cs_ in zip(buffers, copies):
-                for c in cs_[step - 1]:
-                    c.wait_recv()
+            for name, ref in zip(names, buffers):
+                base = bases[step - 1]
+                all_here((name, base), ref.at[pl.ds(base + 1, len(hops[step - 1]))])
                 ref[near + 2 * (step - 1)] = over_hop(ref, step - 1)
         if step < steps - 1:
             for cs_ in copies:
@@ -489,8 +511,8 @@
                     c.start()
 
     def first_sums():
-        for c in t_sum + t_inb:
-            c.wait_recv()
+        all_here("t_sum", tsum.at[others])
+        all_here("t_inb", rinb.at[others])
         parts = []
         for r in range(brow):
             u = natural(r // prow) * prow + r % prow
@@ -501,15 +523,14 @@
         return over_tensor(tsum), jnp.stack(parts)
 
     def first_qv():
-        for c in t_qv:
-            c.wait_recv()
+        all_here("t_qv", tqv.at[others])
         return (over_tensor(tqv),)
 
     def reduce_sums(step):
-        go(step, (sbuf, ibuf), (d_sum, d_inb), first_sums)
+        go(step, ("sum", "inb"), (sbuf, ibuf), (d_sum, d_inb), first_sums)
 
     def reduce_qv(step):
-        go(step, (qbuf,), (d_qv,), first_qv)
+        go(step, ("qv",), (qbuf,), (d_qv,), first_qv)
 
     for c in t_sum + t_inb:
         c.start()
@@ -567,23 +588,31 @@
             for i, ref in enumerate((hid, k, v)):
                 acc += dot_nt(ref[n], qkvw[n + i * tiles, cols(t), :])
         f1[:, cols(t)] = acc
-        pltpu.make_async_copy(f1.at[:, cols(t)], grad_out.at[:, cols(t)], lsem.at[20 + t]).start()
+        pltpu.make_async_copy(f1.at[:, cols(t)], grad_out.at[:, cols(t)], lsem.at[0]).start()
 
     for s in range(1, steps):
         reduce_sums(s)
         reduce_qv(s)
     last = near + 2 * (steps - 2)
-    outs = [load(7, sbuf.at[last], sums_out), load(16, qbuf.at[last], qv_out), load(17, ibuf.at[last], inb_out)]
-
-    for d in far:
-        for c in direct[d] + to_x[d] + to_z[d] + list(pass_on[d].values()):
-            c.wait_send()
-    for c in core_in + [core_ffn] + bias + t_sum + t_inb + t_qv + sum(d_sum + d_inb + d_qv, []):
+    outs = [load(1, sbuf.at[last], sums_out), load(2, qbuf.at[last], qv_out), load(3, ibuf.at[last], inb_out)]
+
+    hops_far = len(far)
+    gone = {"y": 3 * part, "x": part * 5 // 2, "z": part * 5 // 2, "on": 8 * part}
+    for name, size in gone.items():
+        if hops_far:
+            all_gone(name, ffw.at[pl.ds(0, size * hops_far), :])
+    all_gone("core", ffw.at[pl.ds(0, 2 * units), :])
+    for c in bias:
         c.wait_send()
-    c_grad = [pltpu.make_async_copy(f1.at[:, cols(t)], grad_out.at[:, cols(t)], lsem.at[20 + t]) for t in range(tiles)]
-    for c in [c_act] + c_grad + outs:
+    for name, ref in (("t_sum", tsum), ("t_inb", rinb), ("t_qv", tqv)):
+        all_gone(name, ref.at[others])
+    for base, hop in zip(bases, hops):
+        for name, ref in (("sum", sbuf), ("inb", ibuf), ("qv", qbuf)):
+            all_gone((name, base), ref.at[pl.ds(base + 1, len(hop))])
+    pltpu.make_async_copy(f1, grad_out, lsem.at[0]).wait()
+    for c in [c_act] + outs:
         c.wait()
-    assert count[0] <= send.shape[0]
+    assert len(sent) == send.shape[0] and len(got) == recv.shape[0]
 
 
 def finish(act, grad, sums, qv, inb, act_out, grad_out, qv_out, outb_out, shift1_out, inb_out, ffnb_out, shift2_out, abuf, gbuf, sbuf, qbuf, ibuf, into, out):
@@ -625,7 +654,8 @@
     near = min(ranks, 8)
     far_bits = (ranks // near).bit_length() - 1
     slots = near + 2 * far_bits + 1
-    copies = (line - 1) * 36 + units // TILE + 1 + 4 * (group - 1) + 3 * (near - 1 + far_bits)
+    sends = 4 * (line > 1) + 1 + (group - 1) + 3 + 3 * (1 + far_bits)
+    recvs = (line - 1) * 28 + 2 + (group - 1) + 3 + 3 * (1 + far_bits)
     vectors = (type_table, qv_bias, out_bias, gain_one, shift_one, ffn_bias, gain_two, shift_two)
     V = pltpu.VMEM
     outside = pl.BlockSpec(memory_space=pl.ANY)
@@ -676,10 +706,10 @@
             pltpu.SMEM((1, 2), jnp.int32),
             V((rows, LANES), F32),
             V((tiles, TILE, rows), F32),
-            pltpu.SemaphoreType.DMA((3 * tiles + units // TILE,)),
-            pltpu.SemaphoreType.DMA((20 + tiles,)),
-            pltpu.SemaphoreType.DMA((copies,)),
-            pltpu.SemaphoreType.DMA((copies,)),
+            pltpu.SemaphoreType.DMA((4,)),
+            pltpu.SemaphoreType.DMA((15,)),
+            pltpu.SemaphoreType.DMA((sends,)),
+            pltpu.SemaphoreType.DMA((recvs,)),
         ],
         compiler_params=pltpu.CompilerParams(collective_id=0, has_side_effects=True, vmem_limit_bytes=67043328),
     )(
@@ -715,8 +745,8 @@
             V((4, width), F32),
             V((2, width), F32),
             V((brow, 1, LANES), F32),
-            pltpu.SemaphoreType.DMA((16,)),
-            pltpu.SemaphoreType.DMA((16,)),
+            pltpu.SemaphoreType.DMA((11,)),
+            pltpu.SemaphoreType.DMA((15,)),
         ],
     )(act, grad, sums, qv, inb)
     return (

time: 81.4 us -> 80.3 us (0.986)
  Pallas kernels: 79.5 us -> 78.4 us
    pallas_call x1, Pallas kernels: 76.5 us -> 75.5 us  [step(): pl.pallas_call(functools.partial(kernel, ranks, group), out_shape=(jax.Sh...]
where the time goes in v8:
time: 80.3 us; the launch traced here: 79.9 us
  Pallas kernels  78.4 us (98%)
  between operations  1.45 us (2%)
    pallas_call x1, Pallas kernels, step(): pl.pallas_call(functools.partial(kernel, ranks, group), out_shape=(jax.Sh...  75.5 us
    pallas_call x1, Pallas kernels, step(): pl.pallas_call(finish, out_shape=(jax.ShapeDtypeStruct((rows, width), BF1...  2.96 us

profile of v8, /device:TPU:0, one launch (start us, length us, event | category | flops | bytes accessed | tf_op | source)
XLA Modules:
  0.0 79.9 jit_solution(3728921092739108704)
XLA Ops:
  1.3 75.5 %shard_map.224 = (bf16[512,1024]{1,0:T(8,128)(2,1)}, f32[512,1024]{1,0:T(8,128)}, f32[4,1024]{1,0:T(4,128)}, f32[2,1024]{1,0:T(2,128)}, f32[8,1,128]{2,1,0:T(1,128)}) custom-call(s32[1]{0:T(128)S(6)} %copy.25.lengths, s32[1,2]{1,0:T(1,128)} %separators.1, bf16[2,1024]{1,0:T(2,128)(2,1)} %table.1, bf16[2,1024]{1,0:T(2,128)(2,1)} %qv_b.1, ...), custom_call_target="tpu_custom_call" | custom-call | tf_op jit(solution)/shard_map/pallas_call | solution.py:662
  76.7 3.0 %shard_map.225 = (bf16[512,1024]{1,0:T(8,128)(2,1)}, f32[512,1024]{1,0:T(8,128)}, f32[2,1024]{1,0:T(2,128)}, f32[1,1024]{1,0:T(1,128)}, f32[1,1024]{1,0:T(1,128)...) custom-call(bf16[512,1024]{1,0:T(8,128)(2,1)} %get-tuple-element.21.act, ...), custom_call_target="tpu_custom_call" | custom-call | tf_op jit(solution)/shard_map/pallas_call | solution.py:728
